TPU v7x, 32 devices: a whole 2x2x4 slice. The times are simulated.
32 devices in a mesh: rep: 8 (over y, x, core), tp: 4 (over z).
Axes of the slice: x: 2, y: 2, z: 4, core: 2. Of those that a mesh axis runs over, the one named last changes fastest.
Arguments:
- states: bfloat16 [4, 32, 8192], P(None, 'rep'), may hold values from -6 to 6
- norm_gain: float32 [8192], replicated, may hold values from 0.1 to 1.9
- w_query: bfloat16 [8192, 8192], P(('rep', 'tp')), may hold values from -0.0625 to 0.0625
- w_key: bfloat16 [8192, 1024], P(('rep', 'tp')), may hold values from -0.0625 to 0.0625
- w_value: bfloat16 [8192, 1024], P(('rep', 'tp')), may hold values from -0.0625 to 0.0625
- w_out: bfloat16 [8192, 8192], P(None, ('rep', 'tp')), may hold values from -0.0625 to 0.0625
- bias_query: bfloat16 [8192], P('tp'), may hold values from -4 to 4
- bias_key: bfloat16 [1024], P('tp'), may hold values from -4 to 4
- bias_value: bfloat16 [1024], P('tp'), may hold values from -4 to 4
- key_cache: bfloat16 [32, 8, 4096, 128], P('rep', 'tp'), may hold values from -120 to 120
- value_cache: bfloat16 [32, 8, 4096, 128], P('rep', 'tp'), may hold values from -6 to 6
- lengths: int32 [32], P('rep'), may hold values from 1 to 4096, as said below
Outputs:
- mixed: bfloat16 [4, 32, 8192], P(None, 'rep', 'tp')
Inputs may be any that keep to these rules, and one draw needn't show every extreme that they name: `lengths`: each row's number of live cached positions; some row has exactly 4096.
All inputs are finite; a program needn't handle non-finite values.
Results may differ from a plain program's by a relative error of at most 0.0084.
Values may be sent and summed in bfloat16 or wider, within the bound.
A program may use at most 128 MiB of HBM per device.

v0:
```python
import functools

import jax
import jax.numpy as jnp
from jax import lax
from jax.experimental import pallas as pl
from jax.experimental.pallas import tpu as pltpu
from jax.sharding import PartitionSpec as P

THETA = 1000000.0
EPS = 1e-06
MESH = pl.DeviceIdType.MESH
BLK = 1024
TILE = 256


def rotate(vectors, positions, head_size):
    half = head_size // 2
    freqs = THETA ** (-jnp.arange(half, dtype=jnp.float32) * 2.0 / head_size)
    angles = positions.astype(jnp.float32)[..., None, None] * freqs
    first = vectors[..., :half]
    second = vectors[..., half:]
    cosine = jnp.cos(angles)
    sine = jnp.sin(angles)
    return jnp.concatenate(
        [first * cosine - second * sine, second * cosine + first * sine], axis=-1
    )


def remote(src, dst, send, recv, device):
    return pltpu.make_async_remote_copy(
        src_ref=src, dst_ref=dst, send_sem=send, recv_sem=recv,
        device_id=device, device_id_type=MESH,
    )


def project_kernel(
    R, T, x_ref, wq_ref, wk_ref, wv_ref, out_ref,
    xs, wbuf, sendp, recvp, own, send2, recv2, send3, recv3,
    wsem, lsem, xsend, xrecv, psend, precv, s2send, s2recv, s3send, s3recv,
):
    r, t = lax.axis_index("rep"), lax.axis_index("tp")
    half = R // 2
    c, q = lax.rem(r, 2), r // 2
    partner = r + 1 - 2 * c
    rows, depth = x_ref.shape[1], x_ref.shape[2]
    qw, kw = wq_ref.shape[1] // T, wk_ref.shape[1] // T
    cw = qw + 2 * kw

    def target(j):
        return lax.rem(t + 1 + j, T)

    loads = []
    for j in range(T):
        d = target(j)
        group = []
        for i, (ref, width, place) in enumerate(
            ((wq_ref, qw, 0), (wk_ref, kw, qw), (wv_ref, kw, qw + kw))
        ):
            group.append(
                pltpu.make_async_copy(
                    ref.at[:, pl.ds(pl.multiple_of(d * width, width), width)],
                    wbuf.at[j, :, pl.ds(place, width)],
                    wsem.at[j, i],
                )
            )
        loads.append(group)
    for group in loads:
        for copy in group:
            copy.start()
    mine = pltpu.make_async_copy(x_ref.at[r], xs.at[c, q], lsem)
    mine.start()

    barrier = pltpu.get_barrier_semaphore()
    for d in range(1, R):
        pl.semaphore_signal(
            barrier, inc=1, device_id=(lax.rem(r + d, R), t), device_id_type=MESH
        )
    for d in range(1, T):
        pl.semaphore_signal(
            barrier, inc=1, device_id=(r, lax.rem(t + d, T)), device_id_type=MESH
        )
    pl.semaphore_wait(barrier, R + T - 2)

    sends = []
    for d in range(1, R):
        peer = lax.rem(r + d, R)
        copy = remote(x_ref.at[peer], xs.at[c, q], xsend.at[d], xrecv.at[d], (peer, t))
        copy.start()
        sends.append(copy)
    mine.wait()
    for d in range(1, R):
        source = lax.rem(r + R - d, R)
        slot = xs.at[lax.rem(source, 2), source // 2]
        remote(slot, slot, xsend.at[d], xrecv.at[d], (source, t)).wait_recv()

    def first(j):
        for copy in loads[j]:
            copy.wait()

        def tile(i, _):
            cols = pl.ds(pl.multiple_of(i * TILE, TILE), TILE)
            w = wbuf[j, :, cols]
            away = jnp.dot(
                xs[1 - c].reshape(half * rows, depth), w, preferred_element_type=jnp.float32
            )
            sendp[j, :, :, cols] = away.astype(jnp.bfloat16).reshape(half, rows, TILE)
            here = jnp.dot(
                xs[c].reshape(half * rows, depth), w, preferred_element_type=jnp.float32
            )
            own[j, :, :, cols] = here.reshape(half, rows, TILE)
            return 0

        lax.fori_loop(0, cw // TILE, tile, 0)
        copy = remote(sendp.at[j], recvp.at[j], psend.at[j], precv.at[j], (partner, t))
        copy.start()
        sends.append(copy)

    def second(j):
        remote(sendp.at[j], recvp.at[j], psend.at[j], precv.at[j], (partner, t)).wait_recv()
        both = own[j] + recvp[j].astype(jnp.float32)
        own[j] = both
        send2[j] = both.astype(jnp.bfloat16)
        for d in range(1, half):
            to = lax.rem(q + d, half)
            copy = remote(
                send2.at[j, to], recv2.at[j, d], s2send.at[j, d], s2recv.at[j, d], (2 * to + c, t)
            )
            copy.start()
            sends.append(copy)

    def third(j):
        total = own[j, q]
        for d in range(1, half):
            slot = recv2.at[j, d]
            remote(slot, slot, s2send.at[j, d], s2recv.at[j, d], (partner, t)).wait_recv()
            total += slot[...].astype(jnp.float32)
        if j < T - 1:
            send3[j] = total.astype(jnp.bfloat16)
            copy = remote(
                send3.at[j], recv3.at[j], s3send.at[j], s3recv.at[j], (r, target(j))
            )
            copy.start()
            sends.append(copy)
        else:
            out_ref[...] = total

    for step in range(T + 3):
        if step < T:
            first(step)
        if 1 <= step <= T:
            second(step - 1)
        if 3 <= step:
            third(step - 3)
    for j in range(T - 1):
        slot = recv3.at[j]
        remote(slot, slot, s3send.at[j], s3recv.at[j], (partner, t)).wait_recv()
        out_ref[...] += slot[...].astype(jnp.float32)
    for copy in sends:
        copy.wait_send()


def project(R, T, x, w_query, w_key, w_value):
    _, rows, depth = x.shape
    cw = (w_query.shape[1] + w_key.shape[1] + w_value.shape[1]) // T
    half = R // 2
    bf, f32 = jnp.bfloat16, jnp.float32
    dma = pltpu.SemaphoreType.DMA
    any_spec = pl.BlockSpec(memory_space=pl.ANY)
    vmem = pl.BlockSpec(memory_space=pltpu.VMEM)
    return pl.pallas_call(
        functools.partial(project_kernel, R, T),
        out_shape=jax.ShapeDtypeStruct((rows, cw), f32),
        in_specs=[vmem, any_spec, any_spec, any_spec],
        out_specs=vmem,
        scratch_shapes=[
            pltpu.VMEM((2, half, rows, depth), bf),
            pltpu.VMEM((T, depth, cw), bf),
            pltpu.VMEM((T, half, rows, cw), bf),
            pltpu.VMEM((T, half, rows, cw), bf),
            pltpu.VMEM((T, half, rows, cw), f32),
            pltpu.VMEM((T, half, rows, cw), bf),
            pltpu.VMEM((T, half, rows, cw), bf),
            pltpu.VMEM((T, rows, cw), bf),
            pltpu.VMEM((T, rows, cw), bf),
            dma((T, 3)), dma, dma((R,)), dma((R,)), dma((T,)), dma((T,)),
            dma((T, half)), dma((T, half)), dma((T,)), dma((T,)),
        ],
        compiler_params=pltpu.CompilerParams(
            collective_id=0, has_side_effects=True, vmem_limit_bytes=48 << 20
        ),
        name="project",
    )(x, w_query, w_key, w_value)


def attend_kernel(steps, len_ref, q_ref, nk_ref, nv_ref, k_ref, v_ref, o_ref, top, total, accum):
    s = pl.program_id(1)
    length = len_ref[pl.program_id(0)]
    heads, count, head_size = q_ref.shape[1:]
    group = count // steps
    scale = 1.0 / head_size**0.5
    contract = (((1,), (1,)), ((), ()))

    @pl.when(s == 0)
    def _():
        padded = nk_ref.shape[2]
        rank = lax.broadcasted_iota(jnp.int32, (count, padded), 0) // group
        place = lax.broadcasted_iota(jnp.int32, (count, padded), 1)
        for h in range(heads):
            scores = scale * lax.dot_general(
                q_ref[0, h], nk_ref[0, h], contract, preferred_element_type=jnp.float32
            )
            scores = jnp.where(place <= rank, scores, -1e30)
            peak = jnp.max(scores, axis=-1, keepdims=True)
            weights = jnp.where(place <= rank, jnp.exp(scores - peak), 0.0)
            top[h] = jnp.broadcast_to(peak, top.shape[1:])
            total[h] = jnp.broadcast_to(
                jnp.sum(weights, axis=-1, keepdims=True), total.shape[1:]
            )
            accum[h] = jnp.dot(
                weights.astype(jnp.bfloat16), nv_ref[0, h], preferred_element_type=jnp.float32
            )

    @pl.when(s * k_ref.shape[2] < length)
    def _():
        block = k_ref.shape[2]
        place = s * block + lax.broadcasted_iota(jnp.int32, (count, block), 1)
        valid = place < length
        for h in range(heads):
            scores = scale * lax.dot_general(
                q_ref[0, h], k_ref[0, h], contract, preferred_element_type=jnp.float32
            )
            scores = jnp.where(valid, scores, -1e30)
            before = top[h][:, :1]
            fresh = jnp.maximum(before, jnp.max(scores, axis=-1, keepdims=True))
            weights = jnp.where(valid, jnp.exp(scores - fresh), 0.0)
            factor = jnp.exp(before - fresh)
            top[h] = jnp.broadcast_to(fresh, top.shape[1:])
            total[h] = total[h] * factor + jnp.sum(weights, axis=-1, keepdims=True)
            accum[h] = accum[h] * factor + jnp.dot(
                weights.astype(jnp.bfloat16), v_ref[0, h], preferred_element_type=jnp.float32
            )

    @pl.when(s == pl.num_programs(1) - 1)
    def _():
        for h in range(heads):
            o_ref[0, h] = (accum[h] / total[h]).astype(o_ref.dtype)


def attend(query, new_keys, new_values, key_cache, value_cache, lengths):
    steps, rows, heads_q, head_size = query.shape
    heads, context = key_cache.shape[1:3]
    group = heads_q // heads
    count = steps * group
    grouped = query.reshape(steps, rows, heads, group, head_size).transpose(1, 2, 0, 3, 4)
    grouped = grouped.reshape(rows, heads, count, head_size)
    pad = ((0, 0), (0, 0), (0, -steps % 16), (0, 0))
    fresh_keys = jnp.pad(new_keys.transpose(1, 2, 0, 3), pad)
    fresh_values = jnp.pad(new_values.transpose(1, 2, 0, 3), pad)
    block = min(BLK, context)

    def small(b, s, lens):
        return (b, 0, 0, 0)

    def cache(b, s, lens):
        return (b, 0, jnp.minimum(s, (lens[b] - 1) // block), 0)

    padded = fresh_keys.shape[2]
    attended = pl.pallas_call(
        functools.partial(attend_kernel, steps),
        out_shape=jax.ShapeDtypeStruct((rows, heads, count, head_size), jnp.bfloat16),
        grid_spec=pltpu.PrefetchScalarGridSpec(
            num_scalar_prefetch=1,
            grid=(rows, context // block),
            in_specs=[
                pl.BlockSpec((1, heads, count, head_size), small),
                pl.BlockSpec((1, heads, padded, head_size), small),
                pl.BlockSpec((1, heads, padded, head_size), small),
                pl.BlockSpec((1, heads, block, head_size), cache),
                pl.BlockSpec((1, heads, block, head_size), cache),
            ],
            out_specs=pl.BlockSpec((1, heads, count, head_size), small),
            scratch_shapes=[pltpu.VMEM((heads, count, head_size), jnp.float32)] * 3,
        ),
        compiler_params=pltpu.CompilerParams(
            dimension_semantics=("arbitrary", "arbitrary"), vmem_limit_bytes=32 << 20
        ),
        name="attend",
    )(lengths, grouped, fresh_keys, fresh_values, key_cache, value_cache)
    attended = attended.reshape(rows, heads, steps, group, head_size).transpose(2, 0, 1, 3, 4)
    return attended.reshape(steps * rows, heads_q * head_size)


def output_kernel(
    R, T, a_ref, w_ref, out_ref, att, wbuf, acc, obuf, orecv,
    wsem, lsem, zsend, zrecv, csend, crecv, psend, precv, osend, orsem,
):
    r, t = lax.axis_index("rep"), lax.axis_index("tp")
    half, m = R // 2, R // T
    c, q = lax.rem(r, 2), r // 2
    partner = r + 1 - 2 * c
    rows, qw = a_ref.shape
    depth = w_ref.shape[1]
    block = r // m
    slot = lax.rem(r, m) * T + t

    def place(j):
        return lax.rem(t + j, T)

    loads = []
    for j in range(T):
        copy = pltpu.make_async_copy(
            w_ref.at[pl.ds(pl.multiple_of(place(j) * qw, qw), qw), :], wbuf.at[j], wsem.at[j]
        )
        copy.start()
        loads.append(copy)
    mine = pltpu.make_async_copy(a_ref, att.at[t, c, q], lsem.at[0])
    mine.start()

    barrier = pltpu.get_barrier_semaphore()
    for d in range(1, R * T):
        index = lax.rem(r * T + t + d, R * T)
        pl.semaphore_signal(
            barrier, inc=1, device_id=(index // T, lax.rem(index, T)), device_id_type=MESH
        )
    pl.semaphore_wait(barrier, R * T - 1)

    sends = []

    def begin(copy):
        copy.start()
        sends.append(copy)

    for d in range(1, T):
        begin(remote(a_ref, att.at[t, c, q], zsend.at[d], zrecv.at[d], (r, place(d))))
    mine.wait()
    order = [0] + [k for pair in zip(range(T - 1, 0, -1), range(1, T)) for k in pair]
    order = list(dict.fromkeys(order))
    for j in order:
        piece = att.at[place(j), c, q]
        if j:
            d = T - j
            remote(piece, piece, zsend.at[d], zrecv.at[d], (r, place(j))).wait_recv()
        for e in range(1, half):
            to = lax.rem(q + e, half)
            begin(remote(piece, piece, csend.at[j, e], crecv.at[j, e], (2 * to + c, t)))
    for j in order:
        for e in range(1, half):
            piece = att.at[place(j), c, lax.rem(q + half - e, half)]
            remote(piece, piece, csend.at[j, e], crecv.at[j, e], (partner, t)).wait_recv()
        whole = att.at[place(j), c]
        begin(remote(whole, whole, psend.at[j], precv.at[j], (partner, t)))
    for n, j in enumerate(order):
        other = att.at[place(j), 1 - c]
        remote(other, other, psend.at[j], precv.at[j], (partner, t)).wait_recv()
        loads[j].wait()
        part = jnp.dot(
            att[place(j)].reshape(R * rows, qw), wbuf[j], preferred_element_type=jnp.float32
        )
        if n:
            acc[...] += part
        else:
            acc[...] = part
    obuf[...] = acc[...].astype(jnp.bfloat16).reshape(R, rows, depth)
    for d in range(1, R):
        to = lax.rem(r + d, R)
        row = lax.rem(to, 2) * half + to // 2
        begin(remote(obuf.at[row], orecv.at[slot], osend.at[d], orsem.at[slot], (to, block)))
    row = c * half + q

    @pl.when(block == t)
    def _():
        copy = pltpu.make_async_copy(obuf.at[row], orecv.at[slot], orsem.at[slot])
        copy.start()

    @pl.when(block != t)
    def _():
        copy = remote(obuf.at[row], orecv.at[slot], osend.at[0], orsem.at[slot], (r, block))
        copy.start()
        copy.wait_send()

    for s in range(R):
        piece = orecv.at[s]
        pltpu.make_async_copy(piece, piece, orsem.at[s]).wait()
    out_ref[...] = orecv[...]
    for copy in sends:
        copy.wait_send()


def output(R, T, attended, w_out):
    rows, qw = attended.shape
    depth = w_out.shape[1]
    half = R // 2
    bf, f32 = jnp.bfloat16, jnp.float32
    dma = pltpu.SemaphoreType.DMA
    vmem = pl.BlockSpec(memory_space=pltpu.VMEM)
    return pl.pallas_call(
        functools.partial(output_kernel, R, T),
        out_shape=jax.ShapeDtypeStruct((R, rows, depth), bf),
        in_specs=[vmem, pl.BlockSpec(memory_space=pl.ANY)],
        out_specs=vmem,
        scratch_shapes=[
            pltpu.VMEM((T, 2, half, rows, qw), bf),
            pltpu.VMEM((T, qw, depth), bf),
            pltpu.VMEM((R * rows, depth), f32),
            pltpu.VMEM((R, rows, depth), bf),
            pltpu.VMEM((R, rows, depth), bf),
            dma((T,)), dma((1,)), dma((T,)), dma((T,)), dma((T, half)), dma((T, half)),
            dma((T,)), dma((T,)), dma((R,)), dma((R,)),
        ],
        compiler_params=pltpu.CompilerParams(
            collective_id=1, has_side_effects=True, vmem_limit_bytes=48 << 20
        ),
        name="output",
    )(attended, w_out)


def on_device(
    R, T, states, norm_gain, w_query, w_key, w_value, w_out,
    bias_query, bias_key, bias_value, key_cache, value_cache, lengths,
):
    steps, rows, width = states.shape
    head_size = key_cache.shape[3]
    count = steps * rows
    depth = width // (R * T)
    t = lax.axis_index("tp")
    flat = states.reshape(count, width).astype(jnp.float32)
    factor = lax.rsqrt(jnp.mean(flat * flat, axis=-1, keepdims=True) + EPS)
    normed = (flat * factor * norm_gain).astype(jnp.bfloat16)
    blocks = normed.reshape(count, R, T, depth)
    blocks = lax.dynamic_index_in_dim(blocks, t, 2, keepdims=False).transpose(1, 0, 2)
    joined = project(R, T, blocks, w_query, w_key, w_value)
    qw, kw = bias_query.shape[0], bias_key.shape[0]
    bias = jnp.concatenate([bias_query, bias_key, bias_value]).astype(jnp.float32)
    joined = joined + bias
    positions = lengths[None, :] + jnp.arange(steps, dtype=jnp.int32)[:, None]
    heads = joined.reshape(steps, rows, (qw + 2 * kw) // head_size, head_size)
    turned = rotate(heads[:, :, : (qw + kw) // head_size], positions, head_size)
    turned = turned.astype(jnp.bfloat16)
    query = turned[:, :, : qw // head_size]
    keys = turned[:, :, qw // head_size :]
    values = heads[:, :, (qw + kw) // head_size :].astype(jnp.bfloat16)
    attended = attend(query, keys, values, key_cache, value_cache, lengths)
    pieces = output(R, T, attended, w_out)
    summed = pieces.transpose(1, 0, 2).reshape(count, R * depth).astype(jnp.float32)
    residual = lax.dynamic_slice_in_dim(flat, t * summed.shape[1], summed.shape[1], 1)
    return (residual + summed).astype(jnp.bfloat16).reshape(steps, rows, summed.shape[1])


def solution(mesh):
    return jax.shard_map(
        functools.partial(on_device, mesh.shape["rep"], mesh.shape["tp"]),
        mesh=mesh,
        in_specs=(
            P(None, "rep", None), P(), P(("rep", "tp"), None), P(("rep", "tp"), None),
            P(("rep", "tp"), None), P(None, ("rep", "tp")), P("tp"), P("tp"), P("tp"),
            P("rep", "tp", None, None), P("rep", "tp", None, None), P("rep"),
        ),
        out_specs=P(None, "rep", "tp"),
        check_vma=False,
    )
```

profile of v0, /device:TPU:0, one launch (start us, length us, event | category | flops | bytes accessed | tf_op | source)
XLA Modules:
  0.0 92.4 jit_solution(10312463569918844404)
XLA Ops:
  0.0 0.0 copy-start.6
  0.0 0.8 add_convert_fusion.2
  0.8 1.2 %multiply_reduce_fusion = f32[4,4]{1,0:T(4,128)S(1)} fusion(bf16[4,4,8192]{2,1,0:T(4,128)(2,1)} %param.12), kind=kLoop, calls=%fused_computation | loop fusion | flops 393200 | bytes 262208 | tf_op jit(solution)/shard_map/reduce_sum | solution.py:428
  2.0 0.1 rsqrt.12
  2.1 0.7 maximum_convert_fusion
  2.8 0.1 multiply_cosine_fusion
  3.0 0.8 mul.83
  3.8 1.2 %reshape.120 = f32[16,8,4,256]{3,2,1,0:T(4,128)S(1)} reshape(bf16[4,4,8192]{2,1,0:T(4,128)(2,1)} %param.12) | data formatting | bytes 786432 | tf_op jit(solution)/shard_map/convert_element_type | solution.py:427
  5.0 0.1 constant_dynamic-slice_fusion
  5.1 0.1 fusion.3.x_ref
  5.2 0.0 copy-start.2
  5.2 2.2 %copy-done.2 = bf16[256,8192]{1,0:T(8,128)(2,1)S(1)} copy-done((bf16[256,8192]{1,0:T(8,128)(2,1)S(1)}, bf16[256,8192]{1,0:T(8,128)(2,1)}, u32[]{:S(2)}) %copy-start.2) | copy-done | bytes 4194328
  7.4 0.0 copy-start.4
  7.4 1.0 %copy-done.4 = bf16[256,1024]{1,0:T(8,128)(2,1)S(1)} copy-done((bf16[256,1024]{1,0:T(8,128)(2,1)S(1)}, bf16[256,1024]{1,0:T(8,128)(2,1)}, u32[]{:S(2)}) %copy-start.4) | copy-done | bytes 524312
  8.4 0.0 copy-start.5
  8.4 1.0 %copy-done.5 = bf16[256,1024]{1,0:T(8,128)(2,1)S(1)} copy-done((bf16[256,1024]{1,0:T(8,128)(2,1)S(1)}, bf16[256,1024]{1,0:T(8,128)(2,1)}, u32[]{:S(2)}) %copy-start.5) | copy-done | bytes 524312
  9.5 29.9 %project.1 = f32[16,2560]{1,0:T(8,128)S(1)} custom-call(bf16[8,16,256]{2,1,0:T(8,128)(2,1)S(1)} %fusion.3.x_ref, bf16[256,8192]{1,0:T(8,128)(2,1)S(1)} %copy-done.2, bf16[256,1024]{1,0:T(8,128)(2,1)S(1)} %copy-done.4, bf16[256,1024]{1,0:T(8,128)(2,1)S(1)} %copy-done.5), custom_call_target="tpu_custom_call" | custom-call | tf_op jit(solution)/shard_map/project/pallas_call | solution.py:171
  39.5 0.1 fusion.6
  39.6 0.2 add_convert_fusion
  39.8 0.1 fusion.5
  39.9 0.1 fusion.2
  40.1 0.0 copy-done.6
  40.1 0.0 copy-start
  40.1 3.4 %copy-done = bf16[4,2,4096,128]{3,2,1,0:T(8,128)(2,1)S(1)} copy-done((bf16[4,2,4096,128]{3,2,1,0:T(8,128)(2,1)S(1)}, bf16[4,2,4096,128]{3,2,1,0:T(8,128)(2,1)}, u32[]{:S(2)}) %copy-start) | copy-done | bytes 8388632
  43.5 0.0 copy-start.1
  43.5 3.4 %copy-done.1 = bf16[4,2,4096,128]{3,2,1,0:T(8,128)(2,1)S(1)} copy-done((bf16[4,2,4096,128]{3,2,1,0:T(8,128)(2,1)S(1)}, bf16[4,2,4096,128]{3,2,1,0:T(8,128)(2,1)}, u32[]{:S(2)}) %copy-start.1) | copy-done | bytes 8388632
  46.8 0.0 copy-start.7
  46.8 14.8 %attend.1 = bf16[4,2,32,128]{3,2,1,0:T(8,128)(2,1)S(1)} custom-call(s32[4]{0:T(128)S(1)} %copy-done.6, bf16[4,2,32,128]{3,2,1,0:T(8,128)(2,1)S(1)} %bitcast.26, bf16[4,2,16,128]{3,2,1,0:T(8,128)(2,1)S(1)} %pad.7.nk_ref, bf16[4,2,16,128]{3,2,1,0:T(8,128)(2,1)S(1)} %pad.8.nv_ref, bf16[4,2,4096,128]{3,2,1,0:T(8,128)(2,1)S(1)} %copy-done, ...), custom_call_target="tpu_custom_call" | custom-call | tf_op jit(solution)/shard_map/attend/pallas_call | solution.py:269
  61.7 0.0 copy-start.3
  61.7 2.2 %copy-done.3 = bf16[8192,256]{1,0:T(8,128)(2,1)S(1)} copy-done((bf16[8192,256]{1,0:T(8,128)(2,1)S(1)}, bf16[8192,256]{1,0:T(8,128)(2,1)}, u32[]{:S(2)}) %copy-start.3) | copy-done | bytes 4194328
  63.9 27.7 %output.1 = bf16[8,16,256]{2,1,0:T(8,128)(2,1)S(1)} custom-call(bf16[16,2048]{1,0:T(8,128)(2,1)S(1)} %reshape.117.a_ref, bf16[8192,256]{1,0:T(8,128)(2,1)S(1)} %copy-done.3), custom_call_target="tpu_custom_call" | custom-call | tf_op jit(solution)/shard_map/output/pallas_call | solution.py:397
  91.6 0.0 copy-done.7
  91.7 0.7 reshape.118
  (17 shorter events, 0.3 us)
Async XLA Ops:
  0.0 40.1 %copy-start.6 = (s32[4]{0:T(128)S(1)}, s32[4]{0:T(128)}, u32[]{:S(2)}) copy-start(s32[4]{0:T(128)} %len_ref.1) | copy-start | bytes 52
  5.2 2.2 %copy-start.2 = (bf16[256,8192]{1,0:T(8,128)(2,1)S(1)}, bf16[256,8192]{1,0:T(8,128)(2,1)}, u32[]{:S(2)}) copy-start(bf16[256,8192]{1,0:T(8,128)(2,1)} %wq_ref.1) | copy-start | bytes 12582916
  7.4 1.0 %copy-start.4 = (bf16[256,1024]{1,0:T(8,128)(2,1)S(1)}, bf16[256,1024]{1,0:T(8,128)(2,1)}, u32[]{:S(2)}) copy-start(bf16[256,1024]{1,0:T(8,128)(2,1)} %wk_ref.1) | copy-start | bytes 1572868
  8.4 1.0 %copy-start.5 = (bf16[256,1024]{1,0:T(8,128)(2,1)S(1)}, bf16[256,1024]{1,0:T(8,128)(2,1)}, u32[]{:S(2)}) copy-start(bf16[256,1024]{1,0:T(8,128)(2,1)} %wv_ref.1) | copy-start | bytes 1572868
  40.1 3.4 %copy-start = (bf16[4,2,4096,128]{3,2,1,0:T(8,128)(2,1)S(1)}, bf16[4,2,4096,128]{3,2,1,0:T(8,128)(2,1)}, u32[]{:S(2)}) copy-start(bf16[4,2,4096,128]{3,2,1,0:T(8,128)(2,1)} %k_ref.1) | copy-start | bytes 25165828
  43.5 3.4 %copy-start.1 = (bf16[4,2,4096,128]{3,2,1,0:T(8,128)(2,1)S(1)}, bf16[4,2,4096,128]{3,2,1,0:T(8,128)(2,1)}, u32[]{:S(2)}) copy-start(bf16[4,2,4096,128]{3,2,1,0:T(8,128)(2,1)} %v_ref.1) | copy-start | bytes 25165828
  46.8 44.8 %copy-start.7 = (bf16[4,4,8192]{2,1,0:T(4,128)(2,1)S(1)}, bf16[4,4,8192]{2,1,0:T(4,128)(2,1)}, u32[]{:S(2)}) copy-start(bf16[4,4,8192]{2,1,0:T(4,128)(2,1)} %param.12) | copy-start | bytes 786436
  61.7 2.2 %copy-start.3 = (bf16[8192,256]{1,0:T(8,128)(2,1)S(1)}, bf16[8192,256]{1,0:T(8,128)(2,1)}, u32[]{:S(2)}) copy-start(bf16[8192,256]{1,0:T(8,128)(2,1)} %w_ref.1) | copy-start | bytes 12582916
where the time goes:
time: 92.4 us
  Pallas kernels  72.4 us (78%)
  local copies, waits for them, and re-layouts  16.4 us (18%)
  other arithmetic  3.4 us (4%)
    pallas_call x1, Pallas kernels, project(): pl.pallas_call(functools.partial(project_kernel, R, T), out_shape=jax.Sha...  29.9 us
    pallas_call x1, Pallas kernels, output(): pl.pallas_call(functools.partial(output_kernel, R, T), out_shape=jax.Shap...  27.7 us
    pallas_call x1, Pallas kernels, attend(): pl.pallas_call(functools.partial(attend_kernel, steps), out_shape=jax.Sha...  14.8 us
    unnamed x17, local copies, waits for them, and re-layouts  13.2 us

commit v1 on v0

v1 whole, which is shorter than its diff:
```python
import functools

import jax
import jax.numpy as jnp
import numpy as np
from jax import lax
from jax.experimental import pallas as pl
from jax.experimental.pallas import tpu as pltpu
from jax.sharding import PartitionSpec as P

THETA = 1000000.0
EPS = 1e-06
MESH = pl.DeviceIdType.MESH
BLK = 1024
TILE = 256
LOG2E = 1.4426950408889634
CONTRACT = (((1,), (1,)), ((), ()))


def remote(src, dst, send, recv, device):
    return pltpu.make_async_remote_copy(
        src_ref=src, dst_ref=dst, send_sem=send, recv_sem=recv,
        device_id=device, device_id_type=MESH,
    )


def flip(index, mask, size):
    result, bit = 0, 1
    while bit < size:
        digit = lax.rem(index // bit, 2)
        result = result + bit * (1 - digit if mask & bit else digit)
        bit *= 2
    return result


def block_kernel(
    R, T, direct,
    len_ref, freq_ref, x_ref, send_ref, gain_ref, bq_ref, bk_ref, bv_ref,
    wq_ref, wk_ref, wv_ref, wo_ref, kc_ref, vc_ref,
    out_ref,
    xs, xf, xg, ssq, wbuf, wobuf, kbuf, vbuf,
    own, send0, recv0, send1, recv1, send2, recv2, send3, recv3,
    joined, qbuf, knew, vnew, sbuf, abuf, att, acc, obuf,
    wsem, wosem, ksem, vsem, lsem, xsend, xrecv,
    s0s, s0r, s1s, s1r, s2s, s2r, s3s, s3r,
    zsend, zrecv, csend, crecv, psend, precv, osend, orecv, ready,
):
    r, t = lax.axis_index("rep"), lax.axis_index("tp")
    half, X = R // 2, 2
    Y = half // X
    c, q = lax.rem(r, 2), r // 2
    x, y = lax.rem(q, X), q // X
    steps, rows, width = x_ref.shape
    count = steps * rows
    depth = wq_ref.shape[0]
    G = kc_ref.shape[1]
    context, hs = kc_ref.shape[2], kc_ref.shape[3]
    gq = wq_ref.shape[1] // (T * G)
    gh = gq // hs
    cw = gq + 2 * hs
    N = G * T
    bf, f32 = jnp.bfloat16, jnp.float32

    def dev(yy, xx, cc):
        return ((yy * X + xx) * 2 + cc, t)

    partner = dev(y, x, 1 - c)

    def target(j):
        return flip(t, T - 1 - j, T)

    def weights(n):
        g, d = n // T, target(n % T)
        group = []
        for i, (ref, size, place) in enumerate(
            ((wq_ref, gq, 0), (wk_ref, hs, gq), (wv_ref, hs, gq + hs))
        ):
            start = pl.multiple_of((d * G + g) * size, size)
            group.append(
                pltpu.make_async_copy(
                    ref.at[:, pl.ds(start, size)],
                    wbuf.at[n, :, pl.ds(place, size)],
                    wsem.at[n, i],
                )
            )
        return group

    loads = [weights(n) for n in range(N)]
    for group in loads:
        for copy in group:
            copy.start()

    barrier = pltpu.get_barrier_semaphore()
    for d in range(1, R):
        pl.semaphore_signal(
            barrier, inc=1, device_id=(lax.rem(r + d, R), t), device_id_type=MESH
        )
    for d in range(1, T):
        pl.semaphore_signal(
            barrier, inc=1, device_id=(r, lax.rem(t + d, T)), device_id_type=MESH
        )
    pl.semaphore_wait(barrier, R + T - 2)

    sends = []

    def begin(copy):
        copy.start()
        sends.append(copy)

    def features(peer):
        if direct:
            start = pl.multiple_of((peer * T + t) * depth, depth)
            return x_ref.at[:, :, pl.ds(start, depth)]
        return send_ref.at[peer]

    def slot_of(peer):
        qq = peer // 2
        return xs.at[lax.rem(peer, 2), qq // X, lax.rem(qq, X)]

    for d in range(1, R):
        peer = lax.rem(r + d, R)
        begin(remote(features(peer), slot_of(r), xsend.at[d], xrecv.at[d], (peer, t)))
    for d in range(1, T):
        pl.semaphore_signal(
            ready, inc=1, device_id=(r, lax.rem(t + d, T)), device_id_type=MESH
        )

    caches = {}
    for h in range(G):
        for b in range(rows):
            caches[h, b] = (
                pltpu.make_async_copy(kc_ref.at[b, h], kbuf.at[b, h], ksem.at[b, h]),
                pltpu.make_async_copy(vc_ref.at[b, h], vbuf.at[b, h], vsem.at[b, h]),
            )
    outs = [
        pltpu.make_async_copy(wo_ref.at[pl.ds(k * gq, gq), :], wobuf.at[k], wosem.at[k])
        for k in range(N)
    ]

    for i in range(steps):
        value = x_ref[i].astype(f32)
        square = jnp.sum(value * value, axis=-1, keepdims=True)
        ssq[pl.ds(i * rows, rows), :] = jnp.broadcast_to(square, (rows, hs))
    factor = lax.rsqrt(ssq[...] * (1.0 / width) + EPS)
    rank = lax.broadcasted_iota(jnp.int32, (count, hs), 0)
    spot = lax.broadcasted_iota(jnp.int32, (count, hs), 1)
    position = rank // rows
    for b in range(rows):
        position = position + jnp.where(lax.rem(rank, rows) == b, len_ref[b], 0)
    angle = position.astype(f32) * freq_ref[...]
    cosine = jnp.cos(angle)
    sine = jnp.where(spot < hs // 2, -1.0, 1.0) * jnp.sin(angle)

    for d in range(1, R):
        source = lax.rem(r + R - d, R)
        slot = slot_of(source)
        remote(slot, slot, xsend.at[d], xrecv.at[d], (source, t)).wait_recv()
    if direct:
        here = x_ref[:, :, pl.ds(pl.multiple_of((r * T + t) * depth, depth), depth)]
        gain = gain_ref[:, pl.ds(pl.multiple_of((r * T + t) * depth, depth), depth)]
    else:
        here = send_ref[r]
        gain = gain_ref[...]
    xs[c, y, x] = here
    for k in range(2):
        cc = 1 - c if k == 0 else c
        for yy in range(Y):
            for xx in range(X):
                for i in range(steps):
                    at = (((k * Y + yy) * X + xx) * steps + i) * rows
                    xf[pl.ds(at, rows), :] = xs[cc, yy, xx, i].astype(f32)
    xg[...] = (xf[...] * gain).astype(bf)

    def stage0(n):
        for copy in loads[n]:
            copy.wait()

        def tile(i, _):
            cols = pl.ds(pl.multiple_of(i * TILE, TILE), TILE)
            part = jnp.dot(xg[...], wbuf[n, :, cols], preferred_element_type=f32)
            part = part.reshape(2, Y, X, count, TILE)
            send0[n, :, :, :, cols] = part[0].astype(bf)
            own[n, :, :, :, cols] = part[1]
            return 0

        lax.fori_loop(0, cw // TILE, tile, 0)
        begin(remote(send0.at[n], recv0.at[n], s0s.at[n], s0r.at[n], partner))

    def x_first(n):
        return n % 2 == 0

    def stage1(n):
        remote(send0.at[n], recv0.at[n], s0s.at[n], s0r.at[n], partner).wait_recv()
        if x_first(n):
            for yy in range(Y):
                send1[n, yy] = (own[n, yy, 1 - x] + recv0[n, yy, 1 - x].astype(f32)).astype(bf)
            piece = pl.ds(0, Y)
            begin(remote(
                send1.at[n, piece], recv1.at[n, piece], s1s.at[n, 0], s1r.at[n, 0],
                dev(y, 1 - x, c),
            ))
            for yy in range(Y):
                own[n, yy, x] += recv0[n, yy, x].astype(f32)
        else:
            for d in range(1, Y):
                yy = lax.rem(y + d, Y)
                piece = pl.ds((d - 1) * X, X)
                send1[n, piece] = (own[n, yy] + recv0[n, yy].astype(f32)).astype(bf)
                begin(remote(
                    send1.at[n, piece], recv1.at[n, piece], s1s.at[n, d - 1], s1r.at[n, d - 1],
                    dev(yy, x, c),
                ))
            own[n, y] += recv0[n, y].astype(f32)

    def stage2(n):
        if x_first(n):
            piece = pl.ds(0, Y)
            remote(
                send1.at[n, piece], recv1.at[n, piece], s1s.at[n, 0], s1r.at[n, 0], partner
            ).wait_recv()
            for d in range(1, Y):
                yy = lax.rem(y + d, Y)
                send2[n, d - 1] = (own[n, yy, x] + recv1[n, yy].astype(f32)).astype(bf)
                begin(remote(
                    send2.at[n, d - 1], recv2.at[n, d - 1], s2s.at[n, d - 1], s2r.at[n, d - 1],
                    dev(yy, x, c),
                ))
            own[n, y, x] += recv1[n, y].astype(f32)
        else:
            for d in range(1, Y):
                piece = pl.ds((d - 1) * X, X)
                remote(
                    send1.at[n, piece], recv1.at[n, piece], s1s.at[n, d - 1], s1r.at[n, d - 1],
                    partner,
                ).wait_recv()
            away, keep = own[n, y, 1 - x], own[n, y, x]
            for d in range(1, Y):
                away += recv1[n, (d - 1) * X + 1 - x].astype(f32)
                keep += recv1[n, (d - 1) * X + x].astype(f32)
            send2[n, 0] = away.astype(bf)
            begin(remote(
                send2.at[n, 0], recv2.at[n, 0], s2s.at[n, 0], s2r.at[n, 0], dev(y, 1 - x, c)
            ))
            own[n, y, x] = keep

    def stage3(n):
        g, j = n // T, n % T
        total = own[n, y, x]
        for d in range(Y - 1 if x_first(n) else 1):
            slot = recv2.at[n, d]
            remote(slot, slot, s2s.at[n, d], s2r.at[n, d], partner).wait_recv()
            total += slot[...].astype(f32)
        if j < T - 1:
            send3[n] = total.astype(bf)
            begin(remote(
                send3.at[n], recv3.at[n], s3s.at[n], s3r.at[n], (r, target(j))
            ))
        else:
            joined[g] = total

    def turn(value):
        return value * cosine + pltpu.roll(value, hs // 2, 1) * sine

    def stage4(g):
        for j in range(T - 1):
            slot = recv3.at[g * T + j]
            remote(slot, slot, s3s.at[g * T + j], s3r.at[g * T + j], partner).wait_recv()
            joined[g] += slot[...].astype(f32)
        for k in range(gh):
            bias = bq_ref[pl.ds(g * gh + k, 1), :].astype(f32)
            value = joined[g, :, pl.ds(k * hs, hs)] * factor + bias
            qbuf[g, pl.ds(k * count, count), :] = turn(value) * (LOG2E / hs**0.5)
        bias = bk_ref[pl.ds(g, 1), :].astype(f32)
        knew[g] = turn(joined[g, :, pl.ds(gq, hs)] * factor + bias).astype(bf)
        bias = bv_ref[pl.ds(g, 1), :].astype(f32)
        vnew[g] = (joined[g, :, pl.ds(gq + hs, hs)] * factor + bias).astype(bf)

    block = min(BLK, context)
    lines = gh * steps

    def unit(g, b):
        for copy in caches[g, b]:
            copy.wait()
        length = len_ref[b]
        qb = qbuf[g, pl.ds(b, lines, stride=rows), :].astype(bf)
        fresh = lax.dot_general(qb, knew[g], CONTRACT, preferred_element_type=f32)
        asker = lax.rem(lax.broadcasted_iota(jnp.int32, (lines, count), 0), steps)
        place = lax.broadcasted_iota(jnp.int32, (lines, count), 1)
        fine = (lax.rem(place, rows) == b) & (place // rows <= asker)
        fresh = jnp.where(fine, fresh, -1e30)
        peak = jnp.max(fresh, axis=-1, keepdims=True)
        tops = None
        for k in range(context // block):
            part = pl.ds(k * block, block)
            scores = lax.dot_general(qb, kbuf[b, g, part, :], CONTRACT, preferred_element_type=f32)
            where = k * block + lax.broadcasted_iota(jnp.int32, (lines, block), 1)
            scores = jnp.where(where < length, scores, -1e30)
            sbuf[b % 2, :, part] = scores
            for s in range(block // hs):
                piece = scores[:, s * hs : (s + 1) * hs]
                tops = piece if tops is None else jnp.maximum(tops, piece)
        peak = jnp.maximum(peak, jnp.max(tops, axis=-1, keepdims=True))
        weights = jnp.exp2(fresh - peak)
        total = jnp.sum(weights, axis=-1, keepdims=True)
        result = jnp.dot(weights.astype(bf), vnew[g], preferred_element_type=f32)
        sums = None
        for k in range(context // block):
            part = pl.ds(k * block, block)
            weights = jnp.exp2(sbuf[b % 2, :, part] - peak)
            for s in range(block // hs):
                piece = weights[:, s * hs : (s + 1) * hs]
                sums = piece if sums is None else sums + piece
            result += jnp.dot(
                weights.astype(bf), vbuf[b, g, part, :], preferred_element_type=f32
            )
        total = total + jnp.sum(sums, axis=-1, keepdims=True)
        abuf[g, pl.ds(b, lines, stride=rows), :] = result / total

    def attend(g):
        for b in range(rows):
            unit(g, b)
        for k in range(gh):
            att[g, t, c, y, x, :, pl.ds(k * hs, hs)] = abuf[g, pl.ds(k * count, count), :].astype(bf)

    peers = [0] + list(range(T - 1, 0, -1))

    def spread(g):
        mine = att.at[g, t, c, y, x]
        for m in range(1, T):
            begin(remote(mine, mine, zsend.at[g, m], zrecv.at[g, m], (r, flip(t, m, T))))
        across(g, 0)

    def across(g, m):
        piece = att.at[g, flip(t, m, T), c, y, x]
        if m:
            remote(piece, piece, zsend.at[g, m], zrecv.at[g, m], partner).wait_recv()
        for e in range(1, half):
            to = lax.rem(q + e, half)
            begin(remote(
                piece, piece, csend.at[g, m, e], crecv.at[g, m, e], (2 * to + c, t)
            ))

    def collect(g, m):
        for e in range(1, half):
            source = lax.rem(q + half - e, half)
            piece = att.at[g, flip(t, m, T), c, source // X, lax.rem(source, X)]
            remote(piece, piece, csend.at[g, m, e], crecv.at[g, m, e], partner).wait_recv()
        whole = att.at[g, flip(t, m, T), c]
        begin(remote(whole, whole, psend.at[g, m], precv.at[g, m], partner))

    def multiply(g, m, first):
        tt = flip(t, m, T)
        other = att.at[g, tt, 1 - c]
        remote(other, other, psend.at[g, m], precv.at[g, m], partner).wait_recv()
        part = jnp.dot(
            att[g, tt].reshape(R * count, gq), wobuf[tt * G + g], preferred_element_type=f32
        )
        if first:
            acc[...] = part
        else:
            acc[...] += part

    for n in range(N):
        stage0(n)
        if n >= 1:
            stage1(n - 1)
    for h in range(G):
        for b in range(rows):
            for copy in caches[h, b]:
                copy.start()
    for copy in outs:
        copy.start()
    stage1(N - 1)
    for n in range(N + 1):
        if n < N:
            stage2(n)
        if n >= 1:
            stage3(n - 1)
    for g in range(G):
        stage4(g)
        attend(g)
        spread(g)
    for g in range(G):
        for m in peers[1:]:
            across(g, m)
    for copy in outs:
        copy.wait()
    for g in range(G):
        for m in peers:
            collect(g, m)
    for g in range(G):
        for m in peers:
            multiply(g, m, g == 0 and m == 0)

    obuf[...] = acc[...].astype(bf).reshape(obuf.shape)
    block_at = r * T + t
    home, slot = block_at // R, lax.rem(block_at, R)
    pl.semaphore_wait(ready, T - 1)
    for d in range(1, R):
        to = lax.rem(r + d, R)
        qq = to // 2
        piece = obuf.at[lax.rem(to, 2), qq // X, lax.rem(qq, X)]
        begin(remote(piece, out_ref.at[slot], osend.at[d], orecv.at[slot], (to, home)))
    mine = obuf.at[c, y, x]

    @pl.when(home == t)
    def _():
        copy = pltpu.make_async_copy(mine, out_ref.at[slot], orecv.at[slot])
        copy.start()

    @pl.when(home != t)
    def _():
        copy = remote(mine, out_ref.at[slot], osend.at[0], orecv.at[slot], (r, home))
        copy.start()
        copy.wait_send()

    for s in range(R):
        piece = out_ref.at[s]
        pltpu.make_async_copy(piece, piece, orecv.at[s]).wait()
    for copy in sends:
        copy.wait_send()


def on_device(
    R, T, states, norm_gain, w_query, w_key, w_value, w_out,
    bias_query, bias_key, bias_value, key_cache, value_cache, lengths,
):
    steps, rows, width = states.shape
    G, context, hs = key_cache.shape[1:]
    count = steps * rows
    depth = w_query.shape[0]
    columns = w_out.shape[1]
    gq = w_query.shape[1] // (T * G)
    gh = gq // hs
    cw = gq + 2 * hs
    N = G * T
    half, X = R // 2, 2
    Y = half // X
    direct = depth % hs == 0
    t = lax.axis_index("tp")
    at = lax.axis_index("rep") * T + t
    bf, f32 = jnp.bfloat16, jnp.float32
    gain = norm_gain.reshape(1, width)
    sent = states
    if not direct:
        gain = lax.dynamic_slice_in_dim(gain, at * depth, depth, 1)
        sent = states.reshape(steps, rows, R, T, depth)
        sent = lax.dynamic_index_in_dim(sent, t, 3, keepdims=False).transpose(2, 0, 1, 3)
    lane = np.arange(hs) % (hs // 2)
    freqs = (np.float32(THETA) ** (-lane.astype(np.float32) * np.float32(2.0) / np.float32(hs)))
    freqs = jnp.asarray(freqs.astype(np.float32).reshape(1, hs))
    smem = pl.BlockSpec(memory_space=pltpu.SMEM)
    vmem = pl.BlockSpec(memory_space=pltpu.VMEM)
    hbm = pl.BlockSpec(memory_space=pl.ANY)
    dma = pltpu.SemaphoreType.DMA
    V = pltpu.VMEM
    k1, k2 = max(Y, (Y - 1) * X), max(Y - 1, 1)
    pieces = pl.pallas_call(
        functools.partial(block_kernel, R, T, direct),
        out_shape=jax.ShapeDtypeStruct((R, count, columns), bf),
        in_specs=[smem] + [vmem] * 7 + [hbm] * 6,
        out_specs=vmem,
        scratch_shapes=[
            V((2, Y, X, steps, rows, depth), bf), V((R * count, depth), f32),
            V((R * count, depth), bf), V((count, hs), f32),
            V((N, depth, cw), bf), V((N, gq, columns), bf),
            V((rows, G, context, hs), bf), V((rows, G, context, hs), bf),
            V((N, Y, X, count, cw), f32),
            V((N, Y, X, count, cw), bf), V((N, Y, X, count, cw), bf),
            V((N, k1, count, cw), bf), V((N, k1, count, cw), bf),
            V((N, k2, count, cw), bf), V((N, k2, count, cw), bf),
            V((N, count, cw), bf), V((N, count, cw), bf),
            V((G, count, cw), f32), V((G, gh * count, hs), f32),
            V((G, count, hs), bf), V((G, count, hs), bf),
            V((2, gh * steps, context), f32), V((G, gh * count, hs), f32),
            V((G, T, 2, Y, X, count, gq), bf), V((R * count, columns), f32),
            V((2, Y, X, count, columns), bf),
            dma((N, 3)), dma((N,)), dma((rows, G)), dma((rows, G)), dma, dma((R,)), dma((R,)),
            dma((N,)), dma((N,)), dma((N, k1)), dma((N, k1)), dma((N, k2)), dma((N, k2)),
            dma((N,)), dma((N,)),
            dma((G, T)), dma((G, T)), dma((G, T, half)), dma((G, T, half)),
            dma((G, T)), dma((G, T)), dma((R,)), dma((R,)), pltpu.SemaphoreType.REGULAR,
        ],
        compiler_params=pltpu.CompilerParams(
            collective_id=0, has_side_effects=True, vmem_limit_bytes=67043328
        ),
        name="block",
    )(
        lengths, freqs, states, sent, gain,
        bias_query.reshape(-1, hs), bias_key.reshape(-1, hs), bias_value.reshape(-1, hs),
        w_query, w_key, w_value, w_out, key_cache, value_cache,
    )
    share = R * columns
    summed = pieces.reshape(R, steps, rows, columns).transpose(1, 2, 0, 3)
    summed = summed.reshape(steps, rows, share).astype(f32)
    residual = lax.dynamic_slice_in_dim(states, t * share, share, 2).astype(f32)
    return (residual + summed).astype(bf)


def solution(mesh):
    return jax.shard_map(
        functools.partial(on_device, mesh.shape["rep"], mesh.shape["tp"]),
        mesh=mesh,
        in_specs=(
            P(None, "rep", None), P(), P(("rep", "tp"), None), P(("rep", "tp"), None),
            P(("rep", "tp"), None), P(None, ("rep", "tp")), P("tp"), P("tp"), P("tp"),
            P("rep", "tp", None, None), P("rep", "tp", None, None), P("rep"),
        ),
        out_specs=P(None, "rep", "tp"),
        check_vma=False,
    )
```

time: 92.4 us -> 63.1 us (0.68)
  local copies, waits for them, and re-layouts: 16.4 us -> 0.88 us
  Pallas kernels: 72.4 us -> 60.5 us
  other arithmetic: 3.4 us -> 1.51 us
    unnamed x17 -> x0, local copies, waits for them, and re-layouts: 13.2 us -> none
    pallas_call x3 -> x1, Pallas kernels: 72.4 us -> 60.5 us  [on_device(): pl.pallas_call(functools.partial(block_kernel, R, T, direct), out_shape=j...]
    reduce_sum x1 -> x0, other arithmetic: 1.19 us -> none  [on_device(): factor = lax.rsqrt(jnp.mean(flat * flat, axis=-1, keepdims=True) + EPS)]
where the time goes in v1:
time: 63.1 us; the launch traced here: 62.9 us
  Pallas kernels  60.5 us (96%)
  other arithmetic  1.51 us (2%)
  local copies, waits for them, and re-layouts  0.88 us (1%)
    pallas_call x1, Pallas kernels, on_device(): pl.pallas_call(functools.partial(block_kernel, R, T, direct), out_shape=j...  60.5 us
    convert_element_type x1, other arithmetic, on_device(): return (residual + summed).astype(bf)  1.51 us

profile of v1, /device:TPU:0, one launch (start us, length us, event | category | flops | bytes accessed | tf_op | source)
XLA Modules:
  0.0 62.9 jit_solution(1889020746082062938)
XLA Ops:
  0.0 60.5 %block.1 = bf16[8,16,256]{2,1,0:T(8,128)(2,1)} custom-call(s32[4]{0:T(128)} %len_ref.1, f32[1,128]{1,0:T(1,128)} %constant.12.clone.freq_ref, bf16[4,4,8192]{2,1,0:T(4,128)(2,1)} %send_ref.1, bf16[4,4,8192]{2,1,0:T(4,128)(2,1)} %send_ref.1, f32[1,8192]{1,0:T(1,128)} %bitcast.9, bf16[16,128]{1,0:T(8,128)(2,1)} %bitcast.10, bf16[2,128]{1,0:T(2,128)(2,1)} %bitcast.11, ...), custom_call_target="tpu_custom_call" | custom-call | tf_op jit(solution)/shard_map/block/pallas_call | solution.py:458
  60.5 0.9 %reshape.23 = f32[8,4,4,256]{3,2,1,0:T(4,128)S(1)} reshape(bf16[8,16,256]{2,1,0:T(8,128)(2,1)} %block.1) | data formatting | bytes 196608 | tf_op jit(solution)/shard_map/convert_element_type | solution.py:495
  61.4 1.5 %add_convert_fusion = bf16[4,4,2048]{2,1,0:T(4,128)(2,1)} fusion(f32[4,4,2048]{2,1,0:T(4,128)S(1)} %bitcast.7, bf16[4,4,8192]{2,1,0:T(4,128)(2,1)} %send_ref.1, s32[]{:T(128)S(6)} %select_n.3), kind=kLoop, calls=%fused_computation | loop fusion | flops 98304 | bytes 262148 | tf_op jit(solution)/shard_map/convert_element_type | solution.py:497
  (1 shorter events, 0.0 us)

commit v2 on v1

--- a/solution.py
+++ b/solution.py
@@ -13,6 +13,7 @@
 MESH = pl.DeviceIdType.MESH
 BLK = 1024
 TILE = 256
+VMEM_KIB = 61440
 LOG2E = 1.4426950408889634
 CONTRACT = (((1,), (1,)), ((), ()))
 
@@ -35,15 +36,16 @@
 
 def block_kernel(
     R, T, direct,
-    len_ref, freq_ref, x_ref, send_ref, gain_ref, bq_ref, bk_ref, bv_ref,
+    len_ref, freq_hbm, x_hbm, send_hbm, gain_hbm, bq_hbm, bk_hbm, bv_hbm,
     wq_ref, wk_ref, wv_ref, wo_ref, kc_ref, vc_ref,
     out_ref,
+    freq_ref, x_ref, send_ref, gain_ref, bq_ref, bk_ref, bv_ref, pieces,
     xs, xf, xg, ssq, wbuf, wobuf, kbuf, vbuf,
     own, send0, recv0, send1, recv1, send2, recv2, send3, recv3,
     joined, qbuf, knew, vnew, sbuf, abuf, att, acc, obuf,
-    wsem, wosem, ksem, vsem, lsem, xsend, xrecv,
+    wsem, wosem, ksem, vsem, isem, xsend, xrecv,
     s0s, s0r, s1s, s1r, s2s, s2r, s3s, s3r,
-    zsend, zrecv, csend, crecv, psend, precv, osend, orecv, ready,
+    zsend, zrecv, csend, crecv, wsend, wrecv, osend, orecv, ready,
 ):
     r, t = lax.axis_index("rep"), lax.axis_index("tp")
     half, X = R // 2, 2
@@ -59,6 +61,7 @@
     gh = gq // hs
     cw = gq + 2 * hs
     N = G * T
+    columns = wo_ref.shape[1]
     bf, f32 = jnp.bfloat16, jnp.float32
 
     def dev(yy, xx, cc):
@@ -86,9 +89,6 @@
         return group
 
     loads = [weights(n) for n in range(N)]
-    for group in loads:
-        for copy in group:
-            copy.start()
 
     barrier = pltpu.get_barrier_semaphore()
     for d in range(1, R):
@@ -99,6 +99,23 @@
         pl.semaphore_signal(
             barrier, inc=1, device_id=(r, lax.rem(t + d, T)), device_id_type=MESH
         )
+    mine_at = pl.ds(pl.multiple_of((r * T + t) * depth, depth) if direct else 0, depth)
+    small = [
+        pltpu.make_async_copy(src, dst, isem.at[i])
+        for i, (src, dst) in enumerate((
+            (x_hbm, x_ref), (gain_hbm.at[:, mine_at], gain_ref), (freq_hbm, freq_ref),
+            (bq_hbm, bq_ref), (bk_hbm, bk_ref), (bv_hbm, bv_ref), (send_hbm, send_ref),
+        ))
+        if direct is False or dst is not send_ref
+    ]
+    for copy in small:
+        copy.start()
+    for group in loads:
+        for copy in group:
+            copy.start()
+    small[0].wait()
+    if not direct:
+        small[-1].wait()
     pl.semaphore_wait(barrier, R + T - 2)
 
     sends = []
@@ -132,10 +149,16 @@
                 pltpu.make_async_copy(kc_ref.at[b, h], kbuf.at[b, h], ksem.at[b, h]),
                 pltpu.make_async_copy(vc_ref.at[b, h], vbuf.at[b, h], vsem.at[b, h]),
             )
-    outs = [
-        pltpu.make_async_copy(wo_ref.at[pl.ds(k * gq, gq), :], wobuf.at[k], wosem.at[k])
-        for k in range(N)
-    ]
+    outs = []
+    for k in range(N):
+        part = wo_ref.at[pl.ds(k * gq, gq), :]
+        outs.append((
+            pltpu.make_async_copy(part, wobuf.at[c, k], wosem.at[k]),
+            remote(part, wobuf.at[c, k], wsend.at[k], wrecv.at[k], partner),
+        ))
+
+    for copy in small[1:6]:
+        copy.wait()
 
     for i in range(steps):
         value = x_ref[i].astype(f32)
@@ -155,13 +178,7 @@
         source = lax.rem(r + R - d, R)
         slot = slot_of(source)
         remote(slot, slot, xsend.at[d], xrecv.at[d], (source, t)).wait_recv()
-    if direct:
-        here = x_ref[:, :, pl.ds(pl.multiple_of((r * T + t) * depth, depth), depth)]
-        gain = gain_ref[:, pl.ds(pl.multiple_of((r * T + t) * depth, depth), depth)]
-    else:
-        here = send_ref[r]
-        gain = gain_ref[...]
-    xs[c, y, x] = here
+    xs[c, y, x] = x_ref[:, :, mine_at] if direct else send_ref[r]
     for k in range(2):
         cc = 1 - c if k == 0 else c
         for yy in range(Y):
@@ -169,21 +186,18 @@
                 for i in range(steps):
                     at = (((k * Y + yy) * X + xx) * steps + i) * rows
                     xf[pl.ds(at, rows), :] = xs[cc, yy, xx, i].astype(f32)
-    xg[...] = (xf[...] * gain).astype(bf)
+    xg[...] = (xf[...] * gain_ref[...]).astype(bf)
 
     def stage0(n):
         for copy in loads[n]:
             copy.wait()
 
-        def tile(i, _):
-            cols = pl.ds(pl.multiple_of(i * TILE, TILE), TILE)
+        for i in range(cw // TILE):
+            cols = pl.ds(i * TILE, TILE)
             part = jnp.dot(xg[...], wbuf[n, :, cols], preferred_element_type=f32)
             part = part.reshape(2, Y, X, count, TILE)
             send0[n, :, :, :, cols] = part[0].astype(bf)
             own[n, :, :, :, cols] = part[1]
-            return 0
-
-        lax.fori_loop(0, cw // TILE, tile, 0)
         begin(remote(send0.at[n], recv0.at[n], s0s.at[n], s0r.at[n], partner))
 
     def x_first(n):
@@ -316,107 +330,143 @@
         total = total + jnp.sum(sums, axis=-1, keepdims=True)
         abuf[g, pl.ds(b, lines, stride=rows), :] = result / total
 
-    def attend(g):
-        for b in range(rows):
-            unit(g, b)
+    def finish(g):
         for k in range(gh):
-            att[g, t, c, y, x, :, pl.ds(k * hs, hs)] = abuf[g, pl.ds(k * count, count), :].astype(bf)
-
-    peers = [0] + list(range(T - 1, 0, -1))
+            att[g, t, y, x, :, pl.ds(k * hs, hs)] = abuf[g, pl.ds(k * count, count), :].astype(bf)
 
     def spread(g):
-        mine = att.at[g, t, c, y, x]
-        for m in range(1, T):
+        mine = att.at[g, t, y, x]
+        for m in range(T - 1, 0, -1):
             begin(remote(mine, mine, zsend.at[g, m], zrecv.at[g, m], (r, flip(t, m, T))))
         across(g, 0)
 
+    def plane(g, m, yy, xx, k, to):
+        piece = att.at[g, flip(t, m, T), yy, xx]
+        return remote(piece, piece, csend.at[g, m, k], crecv.at[g, m, k], to)
+
     def across(g, m):
-        piece = att.at[g, flip(t, m, T), c, y, x]
         if m:
+            piece = att.at[g, flip(t, m, T), y, x]
             remote(piece, piece, zsend.at[g, m], zrecv.at[g, m], partner).wait_recv()
-        for e in range(1, half):
-            to = lax.rem(q + e, half)
-            begin(remote(
-                piece, piece, csend.at[g, m, e], crecv.at[g, m, e], (2 * to + c, t)
-            ))
+        begin(plane(g, m, y, x, 0, dev(y, 1 - x, c)))
+        for d in range(1, Y):
+            begin(plane(g, m, y, x, d, dev(lax.rem(y + d, Y), x, c)))
+
+    def relay(g, m):
+        if m % 2 == 0:
+            plane(g, m, y, 1 - x, 0, partner).wait_recv()
+            for d in range(1, Y):
+                begin(plane(g, m, y, 1 - x, Y - 1 + d, dev(lax.rem(y + d, Y), x, c)))
+        else:
+            for d in range(1, Y):
+                yy = lax.rem(y + Y - d, Y)
+                plane(g, m, yy, x, d, partner).wait_recv()
+                begin(plane(g, m, yy, x, Y - 1 + d, dev(y, 1 - x, c)))
 
     def collect(g, m):
-        for e in range(1, half):
-            source = lax.rem(q + half - e, half)
-            piece = att.at[g, flip(t, m, T), c, source // X, lax.rem(source, X)]
-            remote(piece, piece, csend.at[g, m, e], crecv.at[g, m, e], partner).wait_recv()
-        whole = att.at[g, flip(t, m, T), c]
-        begin(remote(whole, whole, psend.at[g, m], precv.at[g, m], partner))
-
+        if m % 2:
+            plane(g, m, y, 1 - x, 0, partner).wait_recv()
+        for d in range(1, Y):
+            yy = lax.rem(y + Y - d, Y)
+            if m % 2 == 0:
+                plane(g, m, yy, x, d, partner).wait_recv()
+            plane(g, m, yy, 1 - x, Y - 1 + d, partner).wait_recv()
     def multiply(g, m, first):
         tt = flip(t, m, T)
-        other = att.at[g, tt, 1 - c]
-        remote(other, other, psend.at[g, m], precv.at[g, m], partner).wait_recv()
-        part = jnp.dot(
-            att[g, tt].reshape(R * count, gq), wobuf[tt * G + g], preferred_element_type=f32
-        )
-        if first:
-            acc[...] = part
-        else:
-            acc[...] += part
-
-    for n in range(N):
+        lines = att[g, tt].reshape(half * count, gq)
+        for k in range(2):
+            part = jnp.dot(lines, wobuf[k, tt * G + g], preferred_element_type=f32)
+            if first:
+                acc[k] = part
+            else:
+                acc[k] += part
+
+    early = N // 2
+    for n in range(early):
         stage0(n)
-        if n >= 1:
-            stage1(n - 1)
+    for n in range(early):
+        stage1(n)
+    for n in range(early, N):
+        stage0(n)
     for h in range(G):
         for b in range(rows):
             for copy in caches[h, b]:
                 copy.start()
-    for copy in outs:
+    for copy, swap in outs:
         copy.start()
-    stage1(N - 1)
-    for n in range(N + 1):
-        if n < N:
-            stage2(n)
-        if n >= 1:
-            stage3(n - 1)
+    for p in range(0, N, 2):
+        if p >= 4:
+            stage3(p - 4)
+            stage3(p - 3)
+        stage2(p)
+        stage2(p + 1)
+        if early + p < N:
+            stage1(early + p)
+            stage1(early + p + 1)
+    for n in range(max(N - 4, 0), N):
+        stage3(n)
+    for copy, swap in outs:
+        begin(swap)
     for g in range(G):
         stage4(g)
-        attend(g)
+        for b in range(rows):
+            unit(g, b)
+        finish(g)
         spread(g)
     for g in range(G):
-        for m in peers[1:]:
+        for m in range(1, T):
             across(g, m)
-    for copy in outs:
-        copy.wait()
-    for g in range(G):
-        for m in peers:
-            collect(g, m)
-    for g in range(G):
-        for m in peers:
-            multiply(g, m, g == 0 and m == 0)
+        for m in range(T):
+            relay(g, m)
+        if g == 0:
+            for copy, swap in outs:
+                copy.wait()
+                swap.wait_recv()
+        if g:
+            for m in range(T):
+                collect(g - 1, m)
+                multiply(g - 1, m, g == 1 and m == 0)
+    for m in range(T):
+        collect(G - 1, m)
+        multiply(G - 1, m, G == 1 and m == 0)
 
     obuf[...] = acc[...].astype(bf).reshape(obuf.shape)
-    block_at = r * T + t
-    home, slot = block_at // R, lax.rem(block_at, R)
     pl.semaphore_wait(ready, T - 1)
-    for d in range(1, R):
-        to = lax.rem(r + d, R)
-        qq = to // 2
-        piece = obuf.at[lax.rem(to, 2), qq // X, lax.rem(qq, X)]
-        begin(remote(piece, out_ref.at[slot], osend.at[d], orecv.at[slot], (to, home)))
-    mine = obuf.at[c, y, x]
-
-    @pl.when(home == t)
-    def _():
-        copy = pltpu.make_async_copy(mine, out_ref.at[slot], orecv.at[slot])
-        copy.start()
-
-    @pl.when(home != t)
-    def _():
-        copy = remote(mine, out_ref.at[slot], osend.at[0], orecv.at[slot], (r, home))
-        copy.start()
-        copy.wait_send()
+    for k in range(2):
+        block_at = (2 * q + k) * T + t
+        home, slot = block_at // R, lax.rem(block_at, R)
+        for d in range(1, half):
+            to = lax.rem(q + d, half)
+            begin(remote(
+                obuf.at[k, to // X, lax.rem(to, X)], pieces.at[slot], osend.at[k, d],
+                orecv.at[slot], (2 * to + c, home),
+            ))
+        mine = obuf.at[k, y, x]
+
+        @pl.when(home == t)
+        def _():
+            copy = pltpu.make_async_copy(mine, pieces.at[slot], orecv.at[slot])
+            copy.start()
+
+        @pl.when(home != t)
+        def _():
+            copy = remote(mine, pieces.at[slot], osend.at[k, 0], orecv.at[slot], (r, home))
+            copy.start()
+            copy.wait_send()
 
     for s in range(R):
-        piece = out_ref.at[s]
+        piece = pieces.at[s]
         pltpu.make_async_copy(piece, piece, orecv.at[s]).wait()
+        if direct:
+            value = pieces[s].astype(f32)
+            cols = pl.ds(s * columns, columns)
+            from_x = pl.ds(pl.multiple_of(t * R * columns + s * columns, columns), columns)
+            for i in range(steps):
+                out_ref[i, :, cols] = (
+                    x_ref[i, :, from_x].astype(f32) + value[i * rows : (i + 1) * rows]
+                ).astype(bf)
+        else:
+            out_ref[s] = pieces[s]
     for copy in sends:
         copy.wait_send()
 
@@ -436,7 +486,8 @@
     N = G * T
     half, X = R // 2, 2
     Y = half // X
-    direct = depth % hs == 0
+    direct = depth % hs == 0 and columns % hs == 0
+    share = R * columns
     t = lax.axis_index("tp")
     at = lax.axis_index("rep") * T + t
     bf, f32 = jnp.bfloat16, jnp.float32
@@ -446,24 +497,28 @@
         gain = lax.dynamic_slice_in_dim(gain, at * depth, depth, 1)
         sent = states.reshape(steps, rows, R, T, depth)
         sent = lax.dynamic_index_in_dim(sent, t, 3, keepdims=False).transpose(2, 0, 1, 3)
+    result = (steps, rows, share) if direct else (R, count, columns)
     lane = np.arange(hs) % (hs // 2)
     freqs = (np.float32(THETA) ** (-lane.astype(np.float32) * np.float32(2.0) / np.float32(hs)))
     freqs = jnp.asarray(freqs.astype(np.float32).reshape(1, hs))
     smem = pl.BlockSpec(memory_space=pltpu.SMEM)
     vmem = pl.BlockSpec(memory_space=pltpu.VMEM)
-    hbm = pl.BlockSpec(memory_space=pl.ANY)
+    hbm = pl.BlockSpec(memory_space=pltpu.HBM)
     dma = pltpu.SemaphoreType.DMA
     V = pltpu.VMEM
     k1, k2 = max(Y, (Y - 1) * X), max(Y - 1, 1)
     pieces = pl.pallas_call(
         functools.partial(block_kernel, R, T, direct),
-        out_shape=jax.ShapeDtypeStruct((R, count, columns), bf),
-        in_specs=[smem] + [vmem] * 7 + [hbm] * 6,
+        out_shape=jax.ShapeDtypeStruct(result, bf),
+        in_specs=[smem] + [hbm] * 13,
         out_specs=vmem,
         scratch_shapes=[
+            V((1, hs), f32), V(states.shape, bf), V((8, hs) if direct else sent.shape, bf),
+            V((1, depth), f32), V((G * gh, hs), bf), V((G, hs), bf), V((G, hs), bf),
+            V((R, count, columns), bf),
             V((2, Y, X, steps, rows, depth), bf), V((R * count, depth), f32),
             V((R * count, depth), bf), V((count, hs), f32),
-            V((N, depth, cw), bf), V((N, gq, columns), bf),
+            V((N, depth, cw), bf), V((2, N, gq, columns), bf),
             V((rows, G, context, hs), bf), V((rows, G, context, hs), bf),
             V((N, Y, X, count, cw), f32),
             V((N, Y, X, count, cw), bf), V((N, Y, X, count, cw), bf),
@@ -473,16 +528,16 @@
             V((G, count, cw), f32), V((G, gh * count, hs), f32),
             V((G, count, hs), bf), V((G, count, hs), bf),
             V((2, gh * steps, context), f32), V((G, gh * count, hs), f32),
-            V((G, T, 2, Y, X, count, gq), bf), V((R * count, columns), f32),
+            V((G, T, Y, X, count, gq), bf), V((2, half * count, columns), f32),
             V((2, Y, X, count, columns), bf),
-            dma((N, 3)), dma((N,)), dma((rows, G)), dma((rows, G)), dma, dma((R,)), dma((R,)),
+            dma((N, 3)), dma((N,)), dma((rows, G)), dma((rows, G)), dma((7,)), dma((R,)), dma((R,)),
             dma((N,)), dma((N,)), dma((N, k1)), dma((N, k1)), dma((N, k2)), dma((N, k2)),
             dma((N,)), dma((N,)),
             dma((G, T)), dma((G, T)), dma((G, T, half)), dma((G, T, half)),
-            dma((G, T)), dma((G, T)), dma((R,)), dma((R,)), pltpu.SemaphoreType.REGULAR,
+            dma((N,)), dma((N,)), dma((2, half)), dma((R,)), pltpu.SemaphoreType.REGULAR,
         ],
         compiler_params=pltpu.CompilerParams(
-            collective_id=0, has_side_effects=True, vmem_limit_bytes=67043328
+            collective_id=0, has_side_effects=True, vmem_limit_bytes=VMEM_KIB << 10
         ),
         name="block",
     )(
@@ -490,7 +545,8 @@
         bias_query.reshape(-1, hs), bias_key.reshape(-1, hs), bias_value.reshape(-1, hs),
         w_query, w_key, w_value, w_out, key_cache, value_cache,
     )
-    share = R * columns
+    if direct:
+        return pieces
     summed = pieces.reshape(R, steps, rows, columns).transpose(1, 2, 0, 3)
     summed = summed.reshape(steps, rows, share).astype(f32)
     residual = lax.dynamic_slice_in_dim(states, t * share, share, 2).astype(f32)

time: 63.1 us -> 55.8 us (0.88)
  Pallas kernels: 60.5 us -> 54.2 us
  other arithmetic: 1.51 us -> 0 us
    pallas_call x1, Pallas kernels: 60.5 us -> 54.2 us  [on_device(): pl.pallas_call(functools.partial(block_kernel, R, T, direct), out_shape=j...]
    convert_element_type x1 -> x0, other arithmetic: 1.51 us -> none  [on_device(): return (residual + summed).astype(bf)]
    unnamed x0 -> x1, local copies, waits for them, and re-layouts: none -> 1.49 us
    convert_element_type x2 -> x0, local copies, waits for them, and re-layouts: 0.88 us -> none  [on_device(): summed = summed.reshape(steps, rows, share).astype(f32)]
where the time goes in v2:
time: 55.8 us; the launch traced here: 55.7 us
  Pallas kernels  54.2 us (97%)
  local copies, waits for them, and re-layouts  1.49 us (3%)
    pallas_call x1, Pallas kernels, on_device(): pl.pallas_call(functools.partial(block_kernel, R, T, direct), out_shape=j...  54.2 us
    unnamed x1, local copies, waits for them, and re-layouts  1.49 us

profile of v2, /device:TPU:0, one launch (start us, length us, event | category | flops | bytes accessed | tf_op | source)
XLA Modules:
  0.0 55.7 jit_solution(7568572000548946656)
XLA Ops:
  0.0 54.2 %block.1 = bf16[4,4,2048]{2,1,0:T(4,128)(2,1)} custom-call(s32[4]{0:T(128)} %len_ref.1, f32[1,128]{1,0:T(1,128)} %constant.2.clone.freq_hbm, bf16[4,4,8192]{2,1,0:T(4,128)(2,1)} %send_hbm.1, bf16[4,4,8192]{2,1,0:T(4,128)(2,1)} %send_hbm.1, f32[1,8192]{1,0:T(1,128)} %bitcast.4, bf16[16,128]{1,0:T(8,128)(2,1)} %bitcast.5, bf16[2,128]{1,0:T(2,128)(2,1)} %bitcast.6, ...), custom_call_target="tpu_custom_call" | custom-call | tf_op jit(solution)/shard_map/block/pallas_call | solution.py:510
  54.2 1.5 %copy.15 = bf16[4,4,2048]{2,1,0:T(4,128)(2,1)} copy(bf16[4,4,2048]{2,1,0:T(4,128)(2,1)} %block.1) | data formatting | bytes 131072

commit v3 on v2

v3 whole, which is shorter than its diff:
```python
import functools

import jax
import jax.numpy as jnp
import numpy as np
from jax import lax
from jax.experimental import pallas as pl
from jax.experimental.pallas import tpu as pltpu
from jax.sharding import PartitionSpec as P

THETA = 1000000.0
EPS = 1e-06
MESH = pl.DeviceIdType.MESH
BLK = 1024
TILE = 256
VMEM_KIB = 61440
LOG2E = 1.4426950408889634
CONTRACT = (((1,), (1,)), ((), ()))


def remote(src, dst, send, recv, device):
    return pltpu.make_async_remote_copy(
        src_ref=src, dst_ref=dst, send_sem=send, recv_sem=recv,
        device_id=device, device_id_type=MESH,
    )


def flip(index, mask, size):
    result, bit = 0, 1
    while bit < size:
        digit = lax.rem(index // bit, 2)
        result = result + bit * (1 - digit if mask & bit else digit)
        bit *= 2
    return result


def block_kernel(
    R, T, direct,
    len_hbm, freq_hbm, x_hbm, send_hbm, gain_hbm, bq_hbm, bk_hbm, bv_hbm,
    wq_ref, wk_ref, wv_ref, wo_ref, kc_ref, vc_ref,
    out_ref,
    len_ref, freq_ref, x_ref, send_ref, gain_ref, bq_ref, bk_ref, bv_ref, pieces,
    xs, xf, xg, ssq, wbuf, wobuf, kv,
    own, send0, recv0, send1, recv1, send2, recv2, send3, recv3,
    joined, qbuf, knew, vnew, sbuf, abuf, att, acc, obuf,
    isem, wsem, kvsem, wosem, xsend, xrecv, s0s, s0r, s1s, s1r, s2s, s2r, s3s, s3r,
    zsend, zrecv, csend, crecv, fsend, frecv, wsend, wrecv, osend, orecv, ready,
):
    r, t = lax.axis_index("rep"), lax.axis_index("tp")
    half, X = R // 2, 2
    Y = half // X
    c, q = lax.rem(r, 2), r // 2
    x, y = lax.rem(q, X), q // X
    steps, rows, width = x_ref.shape
    count = steps * rows
    depth = wq_ref.shape[0]
    G = kc_ref.shape[1]
    context, hs = kc_ref.shape[2], kc_ref.shape[3]
    gq = wq_ref.shape[1] // (T * G)
    gh = gq // hs
    cw = gq + 2 * hs
    N = G * T
    columns = wo_ref.shape[1]
    bf, f32 = jnp.bfloat16, jnp.float32

    def dev(yy, xx, cc):
        return ((yy * X + xx) * 2 + cc, t)

    partner = dev(y, x, 1 - c)

    def target(j):
        return flip(t, T - 1 - j, T)

    def weights(n):
        g, d = n // T, target(n % T)
        group = []
        for i, (ref, size, place) in enumerate(
            ((wq_ref, gq, 0), (wk_ref, hs, gq), (wv_ref, hs, gq + hs))
        ):
            start = pl.multiple_of((d * G + g) * size, size)
            group.append(
                pltpu.make_async_copy(
                    ref.at[:, pl.ds(start, size)],
                    wbuf.at[n, :, pl.ds(place, size)],
                    wsem.at[n],
                )
            )
        return group

    loads = [weights(n) for n in range(N)]

    barrier = pltpu.get_barrier_semaphore()
    for d in range(1, R):
        pl.semaphore_signal(
            barrier, inc=1, device_id=(lax.rem(r + d, R), t), device_id_type=MESH
        )
    for d in range(1, T):
        pl.semaphore_signal(
            barrier, inc=1, device_id=(r, lax.rem(t + d, T)), device_id_type=MESH
        )
    mine_at = pl.ds(pl.multiple_of((r * T + t) * depth, depth) if direct else 0, depth)
    small = [
        pltpu.make_async_copy(src, dst, isem.at[i])
        for i, (src, dst) in enumerate((
            (x_hbm, x_ref), (gain_hbm.at[:, mine_at], gain_ref), (freq_hbm, freq_ref),
            (bq_hbm, bq_ref), (bk_hbm, bk_ref), (bv_hbm, bv_ref), (len_hbm, len_ref),
            (send_hbm, send_ref),
        ))
        if direct is False or dst is not send_ref
    ]
    for copy in small:
        copy.start()
    small[0].wait()
    if not direct:
        small[-1].wait()
    for group in loads:
        for copy in group:
            copy.start()
    pl.semaphore_wait(barrier, R + T - 2)

    def here(ref, sem):
        pltpu.make_async_copy(ref, ref, sem).wait()

    def sent(ref, sem):
        remote(ref, ref, sem, xrecv, partner).wait_send()

    def got(ref, sem):
        remote(ref, ref, xsend, sem, partner).wait_recv()

    def features(peer):
        if direct:
            start = pl.multiple_of((peer * T + t) * depth, depth)
            return x_ref.at[:, :, pl.ds(start, depth)]
        return send_ref.at[peer]

    def slot_of(peer):
        return xs.at[lax.rem(peer, 2) * half + peer // 2]

    for d in range(1, R):
        peer = lax.rem(r + d, R)
        remote(features(peer), slot_of(r), xsend, xrecv, (peer, t)).start()
    for d in range(1, T):
        pl.semaphore_signal(
            ready, inc=1, device_id=(r, lax.rem(t + d, T)), device_id_type=MESH
        )

    caches = [
        pltpu.make_async_copy(ref.at[b, h], kv.at[i, b, h], kvsem.at[h])
        for h in range(G)
        for b in range(rows)
        for i, ref in enumerate((kc_ref, vc_ref))
    ]
    outs = []
    for k in range(N):
        part = wo_ref.at[pl.ds(k * gq, gq), :]
        outs.append((
            pltpu.make_async_copy(part, wobuf.at[c, k], wosem),
            remote(part, wobuf.at[c, k], wsend, wrecv, partner),
        ))
    for copy in small[1:7]:
        copy.wait()

    for i in range(steps):
        value = x_ref[i].astype(f32)
        square = jnp.sum(value * value, axis=-1, keepdims=True)
        ssq[pl.ds(i * rows, rows), :] = jnp.broadcast_to(square, (rows, hs))
    factor = lax.rsqrt(ssq[...] * (1.0 / width) + EPS)
    rank = lax.broadcasted_iota(jnp.int32, (count, hs), 0)
    spot = lax.broadcasted_iota(jnp.int32, (count, hs), 1)
    position = rank // rows
    for b in range(rows):
        position = position + jnp.where(lax.rem(rank, rows) == b, len_ref[b], 0)
    angle = position.astype(f32) * freq_ref[...]
    cosine = jnp.cos(angle)
    sine = jnp.where(spot < hs // 2, -1.0, 1.0) * jnp.sin(angle)

    got(xs.at[pl.ds(0, R - 1)], xrecv)
    xs[c * half + q] = x_ref[:, :, mine_at] if direct else send_ref[r]
    for k in range(2):
        cc = 1 - c if k == 0 else c
        for yy in range(Y):
            for xx in range(X):
                for i in range(steps):
                    at = (((k * Y + yy) * X + xx) * steps + i) * rows
                    xf[pl.ds(at, rows), :] = xs[cc * half + yy * X + xx, i].astype(f32)
    xg[...] = (xf[...] * gain_ref[...]).astype(bf)

    def stage0(n):
        here(wbuf.at[n], wsem.at[n])
        for i in range(cw // TILE):
            cols = pl.ds(i * TILE, TILE)
            part = jnp.dot(xg[...], wbuf[n, :, cols], preferred_element_type=f32)
            part = part.reshape(2, Y, X, count, TILE)
            send0[n, :, :, :, cols] = part[0].astype(bf)
            own[n, :, :, :, cols] = part[1]
        remote(send0.at[n], recv0.at[n], s0s, s0r.at[n], partner).start()

    def x_first(n):
        return n % 2 == 0

    def stage1(n):
        got(recv0.at[n], s0r.at[n])
        if x_first(n):
            for yy in range(Y):
                send1[n, yy] = (own[n, yy, 1 - x] + recv0[n, yy, 1 - x].astype(f32)).astype(bf)
            piece = pl.ds(0, Y)
            remote(
                send1.at[n, piece], recv1.at[n, piece], s1s.at[0], s1r.at[n], dev(y, 1 - x, c)
            ).start()
            for yy in range(Y):
                own[n, yy, x] += recv0[n, yy, x].astype(f32)
        else:
            for d in range(1, Y):
                yy = lax.rem(y + d, Y)
                piece = pl.ds((d - 1) * X, X)
                send1[n, piece] = (own[n, yy] + recv0[n, yy].astype(f32)).astype(bf)
                remote(
                    send1.at[n, piece], recv1.at[n, piece], s1s.at[1], s1r.at[n], dev(yy, x, c)
                ).start()
            own[n, y] += recv0[n, y].astype(f32)

    def stage2(n):
        if x_first(n):
            got(recv1.at[n, pl.ds(0, Y)], s1r.at[n])
            for d in range(1, Y):
                yy = lax.rem(y + d, Y)
                send2[n, d - 1] = (own[n, yy, x] + recv1[n, yy].astype(f32)).astype(bf)
                remote(
                    send2.at[n, d - 1], recv2.at[n, d - 1], s2s.at[0], s2r.at[n], dev(yy, x, c)
                ).start()
            own[n, y, x] += recv1[n, y].astype(f32)
        else:
            got(recv1.at[n, pl.ds(0, (Y - 1) * X)], s1r.at[n])
            away, keep = own[n, y, 1 - x], own[n, y, x]
            for d in range(1, Y):
                away += recv1[n, (d - 1) * X + 1 - x].astype(f32)
                keep += recv1[n, (d - 1) * X + x].astype(f32)
            send2[n, 0] = away.astype(bf)
            remote(
                send2.at[n, 0], recv2.at[n, 0], s2s.at[1], s2r.at[n], dev(y, 1 - x, c)
            ).start()
            own[n, y, x] = keep

    def stage3(n):
        g, j = n // T, n % T
        total = own[n, y, x]
        pieces_in = Y - 1 if x_first(n) else 1
        got(recv2.at[n, pl.ds(0, pieces_in)], s2r.at[n])
        for d in range(pieces_in):
            total += recv2[n, d].astype(f32)
        if j < T - 1:
            send3[n] = total.astype(bf)
            remote(send3.at[n], recv3.at[n], s3s, s3r.at[g], (r, target(j))).start()
        else:
            joined[g] = total

    def sums_sent():
        part = pl.ds(0, N // 2)
        sent(xs.at[pl.ds(0, R - 1)], xsend)
        sent(send0, s0s)
        sent(send1.at[part, pl.ds(0, Y)], s1s.at[0])
        sent(send1.at[part, pl.ds(0, (Y - 1) * X)], s1s.at[1])
        sent(send2.at[part, pl.ds(0, Y - 1)], s2s.at[0])
        sent(send2.at[part, pl.ds(0, 1)], s2s.at[1])
        sent(send3.at[pl.ds(0, N - G)], s3s)

    def turn(value):
        return value * cosine + pltpu.roll(value, hs // 2, 1) * sine

    def stage4(g):
        got(recv3.at[pl.ds(g * T, T - 1)], s3r.at[g])
        for j in range(T - 1):
            joined[g] += recv3[g * T + j].astype(f32)
        for k in range(gh):
            bias = bq_ref[pl.ds(g * gh + k, 1), :].astype(f32)
            value = joined[g, :, pl.ds(k * hs, hs)] * factor + bias
            qbuf[g, pl.ds(k * count, count), :] = turn(value) * (LOG2E / hs**0.5)
        bias = bk_ref[pl.ds(g, 1), :].astype(f32)
        knew[g] = turn(joined[g, :, pl.ds(gq, hs)] * factor + bias).astype(bf)
        bias = bv_ref[pl.ds(g, 1), :].astype(f32)
        vnew[g] = (joined[g, :, pl.ds(gq + hs, hs)] * factor + bias).astype(bf)

    block = min(BLK, context)
    lines = gh * steps

    def unit(g, b):
        if b == 0:
            here(kv.at[:, :, g], kvsem.at[g])
        length = len_ref[b]
        qb = qbuf[g, pl.ds(b, lines, stride=rows), :].astype(bf)
        fresh = lax.dot_general(qb, knew[g], CONTRACT, preferred_element_type=f32)
        asker = lax.rem(lax.broadcasted_iota(jnp.int32, (lines, count), 0), steps)
        place = lax.broadcasted_iota(jnp.int32, (lines, count), 1)
        fine = (lax.rem(place, rows) == b) & (place // rows <= asker)
        fresh = jnp.where(fine, fresh, -1e30)
        peak = jnp.max(fresh, axis=-1, keepdims=True)
        tops = None
        for k in range(context // block):
            part = pl.ds(k * block, block)
            scores = lax.dot_general(qb, kv[0, b, g, part, :], CONTRACT, preferred_element_type=f32)
            where = k * block + lax.broadcasted_iota(jnp.int32, (lines, block), 1)
            scores = jnp.where(where < length, scores, -1e30)
            sbuf[b % 2, :, part] = scores
            for s in range(block // hs):
                piece = scores[:, s * hs : (s + 1) * hs]
                tops = piece if tops is None else jnp.maximum(tops, piece)
        peak = jnp.maximum(peak, jnp.max(tops, axis=-1, keepdims=True))
        weights = jnp.exp2(fresh - peak)
        total = jnp.sum(weights, axis=-1, keepdims=True)
        result = jnp.dot(weights.astype(bf), vnew[g], preferred_element_type=f32)
        sums = None
        for k in range(context // block):
            part = pl.ds(k * block, block)
            weights = jnp.exp2(sbuf[b % 2, :, part] - peak)
            for s in range(block // hs):
                piece = weights[:, s * hs : (s + 1) * hs]
                sums = piece if sums is None else sums + piece
            result += jnp.dot(
                weights.astype(bf), kv[1, b, g, part, :], preferred_element_type=f32
            )
        total = total + jnp.sum(sums, axis=-1, keepdims=True)
        abuf[g, pl.ds(b, lines, stride=rows), :] = result / total

    def finish(g):
        for k in range(gh):
            att[g, t, q, :, pl.ds(k * hs, hs)] = abuf[g, pl.ds(k * count, count), :].astype(bf)

    def spread(g):
        mine = att.at[g, t, q]
        for m in range(T - 1, 0, -1):
            remote(mine, mine, zsend.at[g], zrecv.at[g, m], (r, flip(t, m, T))).start()
        across(g, 0)

    def across(g, m):
        piece = att.at[g, flip(t, m, T), q]
        if m:
            got(piece, zrecv.at[g, m])
        for e in range(1, half):
            to = lax.rem(q + e, half)
            remote(piece, piece, csend.at[g], crecv.at[g, m], (2 * to + c, t)).start()

    def forward(g):
        got(att.at[g, t, pl.ds(0, half - 1)], crecv.at[g, 0])
        for e in range(1, half):
            piece = att.at[g, t, lax.rem(q + e, half)]
            remote(piece, piece, fsend.at[g], frecv.at[g], (r, flip(t, 1, T))).start()

    def collect(g, m):
        some = att.at[g, flip(t, m, T), pl.ds(0, half - 1)]
        if m == 1:
            got(att.at[g, flip(t, m, T), q], zrecv.at[g, m])
            got(some, frecv.at[g])
        elif m:
            got(some, crecv.at[g, m])

    def rows_sent(g):
        sent(att.at[g, pl.ds(0, T - 1), 0], zsend.at[g])
        sent(att.at[g, pl.ds(0, T - 1), pl.ds(0, half - 1)], csend.at[g])
        sent(att.at[g, 0, pl.ds(0, half - 1)], fsend.at[g])

    def multiply(g, m, first):
        tt = flip(t, m, T)
        lines = att[g, tt].reshape(half * count, gq)
        for k in range(2):
            part = jnp.dot(lines, wobuf[k, tt * G + g], preferred_element_type=f32)
            if first:
                acc[k] = part
            else:
                acc[k] += part

    early = N // 2
    for n in range(early):
        stage0(n)
    for n in range(early):
        stage1(n)
    for n in range(early, N):
        stage0(n)
    for copy in caches:
        copy.start()
    for copy, swap in outs:
        copy.start()
    for n in range(early, min(early + 2, N)):
        stage1(n)
    for p in range(0, N, 2):
        if p >= 4:
            stage3(p - 4)
            stage3(p - 3)
        stage2(p)
        stage2(p + 1)
        if p >= 2 and early + p < N:
            stage1(early + p)
            stage1(early + p + 1)
    for n in range(max(N - 4, 0), N):
        stage3(n)
    for copy, swap in outs:
        swap.start()
    for g in range(G):
        stage4(g)
        for b in range(rows):
            unit(g, b)
        finish(g)
        spread(g)
    for g in range(G):
        for m in range(2, T):
            across(g, m)
        forward(g)
        if g == 0:
            sums_sent()
            here(wobuf.at[c], wosem)
            got(wobuf.at[1 - c], wrecv)
        if g:
            for m in range(T):
                collect(g - 1, m)
                multiply(g - 1, m, g == 1 and m == 0)
    for m in range(T):
        collect(G - 1, m)
        multiply(G - 1, m, G == 1 and m == 0)

    obuf[...] = acc[...].astype(bf).reshape(obuf.shape)
    pl.semaphore_wait(ready, T - 1)
    homes = []
    for k in range(2):
        block_at = (2 * q + k) * T + t
        home, slot = block_at // R, lax.rem(block_at, R)
        for d in range(1, half):
            to = lax.rem(q + d, half)
            remote(
                obuf.at[k * half + to], pieces.at[slot], osend.at[0], orecv, (2 * to + c, home)
            ).start()
        mine = obuf.at[k * half + q]
        stay = pltpu.make_async_copy(mine, pieces.at[slot], orecv)
        go = remote(mine, pieces.at[slot], osend.at[1 + k], orecv, (r, home))
        homes.append((home, go))

        @pl.when(home == t)
        def _():
            stay.start()

        @pl.when(home != t)
        def _():
            go.start()

    for g in range(G):
        rows_sent(g)
    sent(wobuf.at[0], wsend)
    here(pieces, orecv)

    def give(s):
        if direct:
            value = pieces[s].astype(f32)
            cols = pl.ds(s * columns, columns)
            from_x = pl.ds(pl.multiple_of(t * R * columns + s * columns, columns), columns)
            for i in range(steps):
                out_ref[i, :, cols] = (
                    x_ref[i, :, from_x].astype(f32) + value[i * rows : (i + 1) * rows]
                ).astype(bf)
        else:
            out_ref[s] = pieces[s]

    for s in range(R):
        give(s)
    sent(obuf.at[pl.ds(0, 2 * (half - 1))], osend.at[0])
    for home, go in homes:
        @pl.when(home != t)
        def _(go=go):
            go.wait_send()


def on_device(
    R, T, states, norm_gain, w_query, w_key, w_value, w_out,
    bias_query, bias_key, bias_value, key_cache, value_cache, lengths,
):
    steps, rows, width = states.shape
    G, context, hs = key_cache.shape[1:]
    count = steps * rows
    depth = w_query.shape[0]
    columns = w_out.shape[1]
    gq = w_query.shape[1] // (T * G)
    gh = gq // hs
    cw = gq + 2 * hs
    N = G * T
    half, X = R // 2, 2
    Y = half // X
    direct = depth % hs == 0 and columns % hs == 0
    share = R * columns
    t = lax.axis_index("tp")
    at = lax.axis_index("rep") * T + t
    bf, f32 = jnp.bfloat16, jnp.float32
    gain = norm_gain.reshape(1, width)
    sent = states
    if not direct:
        gain = lax.dynamic_slice_in_dim(gain, at * depth, depth, 1)
        sent = states.reshape(steps, rows, R, T, depth)
        sent = lax.dynamic_index_in_dim(sent, t, 3, keepdims=False).transpose(2, 0, 1, 3)
    result = (steps, rows, share) if direct else (R, count, columns)
    lane = np.arange(hs) % (hs // 2)
    freqs = (np.float32(THETA) ** (-lane.astype(np.float32) * np.float32(2.0) / np.float32(hs)))
    freqs = jnp.asarray(freqs.astype(np.float32).reshape(1, hs))
    vmem = pl.BlockSpec(memory_space=pltpu.VMEM)
    hbm = pl.BlockSpec(memory_space=pltpu.HBM)
    dma = pltpu.SemaphoreType.DMA
    V = pltpu.VMEM
    k1, k2 = max(Y, (Y - 1) * X), max(Y - 1, 1)
    pieces = pl.pallas_call(
        functools.partial(block_kernel, R, T, direct),
        out_shape=pltpu.VMEM(result, bf),
        in_specs=[hbm] * 14,
        out_specs=vmem,
        scratch_shapes=[
            pltpu.SMEM((rows,), jnp.int32), V((1, hs), f32), V(states.shape, bf), V((8, hs) if direct else sent.shape, bf),
            V((1, depth), f32), V((G * gh, hs), bf), V((G, hs), bf), V((G, hs), bf),
            V((R, count, columns), bf),
            V((R, steps, rows, depth), bf), V((R * count, depth), f32),
            V((R * count, depth), bf), V((count, hs), f32),
            V((N, depth, cw), bf), V((2, N, gq, columns), bf),
            V((2, rows, G, context, hs), bf),
            V((N, Y, X, count, cw), f32),
            V((N, Y, X, count, cw), bf), V((N, Y, X, count, cw), bf),
            V((N, k1, count, cw), bf), V((N, k1, count, cw), bf),
            V((N, k2, count, cw), bf), V((N, k2, count, cw), bf),
            V((N, count, cw), bf), V((N, count, cw), bf),
            V((G, count, cw), f32), V((G, gh * count, hs), f32),
            V((G, count, hs), bf), V((G, count, hs), bf),
            V((2, gh * steps, context), f32), V((G, gh * count, hs), f32),
            V((G, T, half, count, gq), bf), V((2, half * count, columns), f32),
            V((2 * half, count, columns), bf),
            dma((8,)), dma((N,)), dma((G,)), dma, dma, dma, dma, dma((N,)), dma((2,)), dma((N,)),
            dma((2,)), dma((N,)), dma, dma((G,)),
            dma((G,)), dma((G, T)), dma((G,)), dma((G, T)), dma((G,)), dma((G,)), dma, dma,
            dma((3,)), dma, pltpu.SemaphoreType.REGULAR,
        ],
        compiler_params=pltpu.CompilerParams(
            collective_id=0, has_side_effects=True, vmem_limit_bytes=VMEM_KIB << 10
        ),
        name="block",
    )(
        *(
            pltpu.with_memory_space_constraint(value, pltpu.HBM)
            for value in (
                lengths, freqs, states, sent, gain,
                bias_query.reshape(-1, hs), bias_key.reshape(-1, hs), bias_value.reshape(-1, hs),
                w_query, w_key, w_value, w_out, key_cache, value_cache,
            )
        )
    )
    if direct:
        return pieces
    summed = pieces.reshape(R, steps, rows, columns).transpose(1, 2, 0, 3)
    summed = summed.reshape(steps, rows, share).astype(f32)
    residual = lax.dynamic_slice_in_dim(states, t * share, share, 2).astype(f32)
    return (residual + summed).astype(bf)


def solution(mesh):
    return jax.shard_map(
        functools.partial(on_device, mesh.shape["rep"], mesh.shape["tp"]),
        mesh=mesh,
        in_specs=(
            P(None, "rep", None), P(), P(("rep", "tp"), None), P(("rep", "tp"), None),
            P(("rep", "tp"), None), P(None, ("rep", "tp")), P("tp"), P("tp"), P("tp"),
            P("rep", "tp", None, None), P("rep", "tp", None, None), P("rep"),
        ),
        out_specs=P(None, "rep", "tp"),
        check_vma=False,
    )
```

time: 55.8 us -> 45.8 us (0.82)
  Pallas kernels: 54.2 us -> 45 us
  local copies, waits for them, and re-layouts: 1.49 us -> 0.63 us
    pallas_call x1, Pallas kernels: 54.2 us -> 45 us  [on_device(): pl.pallas_call(functools.partial(block_kernel, R, T, direct), out_shape=p...]
    unnamed x1, local copies, waits for them, and re-layouts: 1.49 us -> 0.63 us
where the time goes in v3:
time: 45.8 us; the launch traced here: 45.6 us
  Pallas kernels  45 us (98%)
  local copies, waits for them, and re-layouts  0.63 us (1%)
    pallas_call x1, Pallas kernels, on_device(): pl.pallas_call(functools.partial(block_kernel, R, T, direct), out_shape=p...  45 us

profile of v3, /device:TPU:0, one launch (start us, length us, event | category | flops | bytes accessed | tf_op | source)
XLA Modules:
  0.0 45.6 jit_solution(11647785937586204698)
XLA Ops:
  0.0 45.0 %block.1 = bf16[4,4,2048]{2,1,0:T(4,128)(2,1)S(1)} custom-call(s32[4]{0:T(128)} %len_hbm.1, f32[1,128]{1,0:T(1,128)} %constant.2.clone.freq_hbm, bf16[4,4,8192]{2,1,0:T(4,128)(2,1)} %send_hbm.1, bf16[4,4,8192]{2,1,0:T(4,128)(2,1)} %send_hbm.1, f32[1,8192]{1,0:T(1,128)} %bitcast.4, bf16[16,128]{1,0:T(8,128)(2,1)} %bitcast.5, bf16[2,128]{1,0:T(2,128)(2,1)} %bitcast.6, ...), custom_call_target="tpu_custom_call" | custom-call | tf_op jit(solution)/shard_map/block/pallas_call | solution.py:504
  45.0 0.6 %copy.15 = bf16[4,4,2048]{2,1,0:T(4,128)(2,1)} copy(bf16[4,4,2048]{2,1,0:T(4,128)(2,1)S(1)} %block.1) | data formatting | bytes 131072

commit v4 on v3

--- a/solution.py
+++ b/solution.py
@@ -11,7 +11,7 @@
 THETA = 1000000.0
 EPS = 1e-06
 MESH = pl.DeviceIdType.MESH
-BLK = 1024
+BLK = 2048
 TILE = 256
 VMEM_KIB = 61440
 LOG2E = 1.4426950408889634
@@ -283,43 +283,59 @@
     block = min(BLK, context)
     lines = gh * steps
 
-    def unit(g, b):
-        if b == 0:
-            here(kv.at[:, :, g], kvsem.at[g])
-        length = len_ref[b]
+    def begin(g, b):
         qb = qbuf[g, pl.ds(b, lines, stride=rows), :].astype(bf)
         fresh = lax.dot_general(qb, knew[g], CONTRACT, preferred_element_type=f32)
         asker = lax.rem(lax.broadcasted_iota(jnp.int32, (lines, count), 0), steps)
         place = lax.broadcasted_iota(jnp.int32, (lines, count), 1)
         fine = (lax.rem(place, rows) == b) & (place // rows <= asker)
-        fresh = jnp.where(fine, fresh, -1e30)
-        peak = jnp.max(fresh, axis=-1, keepdims=True)
-        tops = None
-        for k in range(context // block):
-            part = pl.ds(k * block, block)
-            scores = lax.dot_general(qb, kv[0, b, g, part, :], CONTRACT, preferred_element_type=f32)
-            where = k * block + lax.broadcasted_iota(jnp.int32, (lines, block), 1)
-            scores = jnp.where(where < length, scores, -1e30)
-            sbuf[b % 2, :, part] = scores
-            for s in range(block // hs):
-                piece = scores[:, s * hs : (s + 1) * hs]
-                tops = piece if tops is None else jnp.maximum(tops, piece)
-        peak = jnp.maximum(peak, jnp.max(tops, axis=-1, keepdims=True))
-        weights = jnp.exp2(fresh - peak)
-        total = jnp.sum(weights, axis=-1, keepdims=True)
-        result = jnp.dot(weights.astype(bf), vnew[g], preferred_element_type=f32)
-        sums = None
-        for k in range(context // block):
-            part = pl.ds(k * block, block)
-            weights = jnp.exp2(sbuf[b % 2, :, part] - peak)
-            for s in range(block // hs):
-                piece = weights[:, s * hs : (s + 1) * hs]
-                sums = piece if sums is None else sums + piece
-            result += jnp.dot(
-                weights.astype(bf), kv[1, b, g, part, :], preferred_element_type=f32
-            )
-        total = total + jnp.sum(sums, axis=-1, keepdims=True)
-        abuf[g, pl.ds(b, lines, stride=rows), :] = result / total
+        return {"g": g, "b": b, "q": qb, "fresh": jnp.where(fine, fresh, -1e30)}
+
+    def score(u, k):
+        g, b, part = u["g"], u["b"], pl.ds(k * block, block)
+        scores = lax.dot_general(
+            u["q"], kv[0, b, g, part, :], CONTRACT, preferred_element_type=f32
+        )
+        where = k * block + lax.broadcasted_iota(jnp.int32, (lines, block), 1)
+        scores = jnp.where(where < len_ref[b], scores, -1e30)
+        sbuf[b % 2, :, part] = scores
+        for s in range(block // hs):
+            piece = scores[:, s * hs : (s + 1) * hs]
+            u["tops"] = jnp.maximum(u["tops"], piece) if "tops" in u else piece
+
+    def settle(u):
+        peak = jnp.max(u["fresh"], axis=-1, keepdims=True)
+        u["peak"] = jnp.maximum(peak, jnp.max(u["tops"], axis=-1, keepdims=True))
+        weights = jnp.exp2(u["fresh"] - u["peak"])
+        u["total"] = jnp.sum(weights, axis=-1, keepdims=True)
+        u["result"] = jnp.dot(weights.astype(bf), vnew[u["g"]], preferred_element_type=f32)
+
+    def weigh(u, k):
+        g, b, part = u["g"], u["b"], pl.ds(k * block, block)
+        weights = jnp.exp2(sbuf[b % 2, :, part] - u["peak"])
+        for s in range(block // hs):
+            piece = weights[:, s * hs : (s + 1) * hs]
+            u["sums"] = u["sums"] + piece if "sums" in u else piece
+        u["result"] += jnp.dot(
+            weights.astype(bf), kv[1, b, g, part, :], preferred_element_type=f32
+        )
+
+    def attend(g):
+        here(kv.at[:, :, g], kvsem.at[g])
+        blocks = range(context // block)
+        now = begin(g, 0)
+        for k in blocks:
+            score(now, k)
+        for b in range(rows):
+            later = begin(g, b + 1) if b < rows - 1 else None
+            settle(now)
+            for k in blocks:
+                if later:
+                    score(later, k)
+                weigh(now, k)
+            total = now["total"] + jnp.sum(now["sums"], axis=-1, keepdims=True)
+            abuf[g, pl.ds(b, lines, stride=rows), :] = now["result"] / total
+            now = later
 
     def finish(g):
         for k in range(gh):
@@ -396,14 +412,13 @@
         swap.start()
     for g in range(G):
         stage4(g)
-        for b in range(rows):
-            unit(g, b)
+        attend(g)
         finish(g)
         spread(g)
     for g in range(G):
+        forward(g)
         for m in range(2, T):
             across(g, m)
-        forward(g)
         if g == 0:
             sums_sent()
             here(wobuf.at[c], wosem)

time: 45.8 us -> 45 us (0.983)
  Pallas kernels: 45 us -> 44.2 us
    pallas_call x1, Pallas kernels: 45 us -> 44.2 us  [on_device(): pl.pallas_call(functools.partial(block_kernel, R, T, direct), out_shape=p...]
where the time goes in v4:
time: 45 us; the launch traced here: 44.9 us
  Pallas kernels  44.2 us (98%)
  local copies, waits for them, and re-layouts  0.63 us (1%)
    pallas_call x1, Pallas kernels, on_device(): pl.pallas_call(functools.partial(block_kernel, R, T, direct), out_shape=p...  44.2 us

profile of v4, /device:TPU:0, one launch (start us, length us, event | category | flops | bytes accessed | tf_op | source)
XLA Modules:
  0.0 44.9 jit_solution(7239685035321434127)
XLA Ops:
  0.0 44.2 %block.1 = bf16[4,4,2048]{2,1,0:T(4,128)(2,1)S(1)} custom-call(s32[4]{0:T(128)} %len_hbm.1, f32[1,128]{1,0:T(1,128)} %constant.2.clone.freq_hbm, bf16[4,4,8192]{2,1,0:T(4,128)(2,1)} %send_hbm.1, bf16[4,4,8192]{2,1,0:T(4,128)(2,1)} %send_hbm.1, f32[1,8192]{1,0:T(1,128)} %bitcast.4, bf16[16,128]{1,0:T(8,128)(2,1)} %bitcast.5, bf16[2,128]{1,0:T(2,128)(2,1)} %bitcast.6, ...), custom_call_target="tpu_custom_call" | custom-call | tf_op jit(solution)/shard_map/block/pallas_call | solution.py:519
  44.2 0.6 %copy.15 = bf16[4,4,2048]{2,1,0:T(4,128)(2,1)} copy(bf16[4,4,2048]{2,1,0:T(4,128)(2,1)S(1)} %block.1) | data formatting | bytes 131072
